TPU v7x, 32 devices: a whole 2x2x4 slice. The times are simulated.
32 devices in a mesh: gx: 4 (over x, core), gy: 4 (over z), gz: 2 (over y).
Axes of the slice: x: 2, y: 2, z: 4, core: 2. Of those that a mesh axis runs over, the one named last changes fastest.
Arguments:
- grad_bucket: bfloat16 [32, 1, 3584, 1024], P(('gx', 'gy', 'gz')), may hold values from -72000 to 72000
- parameters: bfloat16 [1, 3584, 1024], P(None, ('gx', 'gy', 'gz')), may hold values from -4 to 4
- row_state: float32 [1, 3584], P(None, ('gx', 'gy', 'gz')), may hold values from 0.01 to 10
- column_state: float32 [1, 1024], replicated, may hold values from 0.01 to 10
Outputs:
- new_parameters: bfloat16 [1, 3584, 1024], P(None, ('gx', 'gy', 'gz'))
- row_next: float32 [1, 3584], P(None, ('gx', 'gy', 'gz'))
- column_next: float32 [1, 1024], replicated
- first_layer: bfloat16 [3584, 1024], replicated
All inputs are finite; a program needn't handle non-finite values.
Results may differ from a plain program's by a relative error of at most 0.011.
Values may be sent and summed in bfloat16 or wider, within the bound.
A program may use at most 128 MiB of HBM per device.

v0:
```python
import functools
import math

import jax
import jax.numpy as jnp
from jax import lax
from jax.experimental import pallas as pl
from jax.experimental.pallas import tpu as pltpu
from jax.sharding import PartitionSpec as P

beta_two = 0.8
step_size = 0.5
AXES = ("gx", "gy", "gz")
TILE = 16
VMEM_BYTES = 67043328 - 131072


def shards(grad_bucket, parameters, row_state, column_state):
    local_grad = grad_bucket[0].astype(jnp.float32)
    layer_count, full_width, columns = local_grad.shape
    summed = lax.psum_scatter(local_grad, AXES, scatter_dimension=1, tiled=True)
    clip_level = 0.5 * math.sqrt(layer_count * full_width * columns)
    squares = summed * summed
    norm_square = lax.psum(jnp.sum(squares), AXES)
    factor = jnp.minimum(jnp.float32(1.0), clip_level / jnp.sqrt(norm_square + 1e-06))
    clipped = factor * summed
    clipped_square = clipped * clipped
    row_next = beta_two * row_state + (1.0 - beta_two) * jnp.mean(clipped_square, axis=2)
    column_part, row_total = lax.psum((jnp.sum(clipped_square, axis=1), jnp.sum(row_next, axis=1)), AXES)
    column_next = beta_two * column_state + (1.0 - beta_two) * column_part / full_width
    row_average = row_total / full_width
    second = row_next[:, :, None] * column_next[:, None, :] / row_average[:, None, None]
    update = clipped / jnp.sqrt(second)
    new_parameters = (parameters.astype(jnp.float32) - step_size * update).astype(jnp.bfloat16)
    first_layer = lax.all_gather(new_parameters[0], AXES, axis=0, tiled=True)
    return (new_parameters, row_next, column_next, first_layer)


def flip(index, mask, size):
    out, bit = 0, 1
    while bit < size:
        out = out + bit * (((index // bit) % 2 + (mask // bit) % 2) % 2)
        bit *= 2
    return out


def kernel(nx, nz, grad, params_in, row_in, col_in, new_ref, row_ref, col_ref, full,
           lg, cr, r1a, r1b, r2a, r2b, rz, summed, own, st, st1, tot, st2, params, row_state, col_state,
           lsem, isem, cs, crv, fas, far, fbs, fbr, gas, gar, gbs, gbr, has, har, hbs, hbr, zs, zr,
           s1s, s1r, s2s, s2r, gzs, gzr, q1as, q1ar, q1bs, q1br, q2as, q2ar, q2bs, q2br,
           q3as, q3ar, q3bs, q3br, gcs, gcr):
    gx, z, y = lax.axis_index("gx"), lax.axis_index("gy"), lax.axis_index("gz")
    x, c = gx // 2, gx % 2
    rows, columns = params.shape
    half = columns // 2
    full_width = rows * 4 * nz * 2
    core_peer = (x * 2 + 1 - c, z, y)
    x_peer = ((1 - x) * 2 + c, z, y)
    y_peer = (gx, z, 1 - y)
    lo, hi = pl.ds(0, half), pl.ds(half, half)
    tiles = rows // TILE
    f32 = jnp.float32
    blocks = [(1 - x, 1 - y), (1 - x, y), (x, 1 - y), (x, y)]

    def zof(t):
        return flip(z, t, nz)

    def rdma(src, dst, ssem, rsem, peer):
        return pltpu.make_async_remote_copy(
            src_ref=src, dst_ref=dst, send_sem=ssem, recv_sem=rsem,
            device_id=peer, device_id_type=pl.DeviceIdType.MESH)

    rs_order = [2, 3, 1, 0] if nz == 4 else list(range(nz - 1, -1, -1))
    loads = {t: pltpu.make_async_copy(grad.at[:, c, zof(t)], lg.at[t], lsem.at[t]) for t in rs_order}
    for t in rs_order:
        loads[t].start()
    small = [pltpu.make_async_copy(src, dst, isem.at[k]) for k, (src, dst) in enumerate(
        [(params_in, params), (row_in, row_state), (col_in, col_state)])]
    for copy in small:
        copy.start()

    barrier = pltpu.get_barrier_semaphore()
    plane = [((gx + a) % nx, z, (y + b) % 2) for a in range(nx) for b in range(2) if (a, b) != (0, 0)]
    line = [(gx, zof(t), y) for t in range(1, nz)]
    for peer in line + plane:
        pl.semaphore_signal(barrier, inc=1, device_id=peer, device_id_type=pl.DeviceIdType.MESH)
    pl.semaphore_wait(barrier, len(plane) + len(line))

    core, fa, fb, ga, gb, ha, hb, zc = {}, {}, {}, {}, {}, {}, {}, {}
    for t in rs_order:
        for k, (bx, by) in enumerate(blocks):
            core[t, k] = rdma(grad.at[bx, 1 - c, zof(t), by], cr.at[t, k], cs.at[t, k], crv.at[t, k], core_peer)
            core[t, k].start()
        fa[t] = rdma(lg.at[t, 1 - x, 1 - y, :, lo], r1a.at[t, 0], fas.at[t], far.at[t], x_peer)
        fb[t] = rdma(lg.at[t, 1 - x, 1 - y, :, hi], r1b.at[t, 0], fbs.at[t], fbr.at[t], y_peer)
        ga[t] = rdma(lg.at[t, 1 - x, y, :, lo], r1a.at[t, 1], gas.at[t], gar.at[t], x_peer)
        gb[t] = rdma(lg.at[t, x, 1 - y, :, hi], r1b.at[t, 1], gbs.at[t], gbr.at[t], y_peer)
        ha[t] = rdma(lg.at[t, x, 1 - y, :, lo], r2a.at[t], has.at[t], har.at[t], y_peer)
        hb[t] = rdma(lg.at[t, 1 - x, y, :, hi], r2b.at[t], hbs.at[t], hbr.at[t], x_peer)
        if t:
            zc[t] = rdma(lg.at[t, x, y], rz.at[t], zs.at[t], zr.at[t], (gx, zof(t), y))

    def add(*terms):
        total = terms[0].astype(f32)
        for term in terms[1:]:
            total = total + term.astype(f32)
        return total

    def over_rows(step):
        @pl.loop(0, tiles, unroll=True)
        def _(i):
            step(pl.ds(pl.multiple_of(i * TILE, TILE), TILE))

    def stage_core(t):
        loads[t].wait()
        for k, (bx, by) in enumerate(blocks):
            core[t, k].wait_recv()

            def step(r):
                lg[t, bx, by, r, :] = add(lg[t, bx, by, r, :], cr[t, k, r, :]).astype(jnp.bfloat16)
            over_rows(step)
            if k == 0:
                fa[t].start()
                fb[t].start()
            elif k == 1:
                ga[t].start()
            elif k == 2:
                gb[t].start()

    def stage_first(t):
        fa[t].wait_recv()
        fb[t].wait_recv()

        def step(r):
            lg[t, x, 1 - y, r, lo] = add(lg[t, x, 1 - y, r, lo], r1a[t, 0, r, :]).astype(jnp.bfloat16)
            lg[t, 1 - x, y, r, hi] = add(lg[t, 1 - x, y, r, hi], r1b[t, 0, r, :]).astype(jnp.bfloat16)
        over_rows(step)
        ha[t].start()
        hb[t].start()

    def stage_second(t):
        for copy in (ga[t], gb[t], ha[t], hb[t]):
            copy.wait_recv()
        if t == 0:
            return

        def step(r):
            lg[t, x, y, r, lo] = add(lg[t, x, y, r, lo], r1a[t, 1, r, :], r2a[t, r, :]).astype(jnp.bfloat16)
            lg[t, x, y, r, hi] = add(lg[t, x, y, r, hi], r1b[t, 1, r, :], r2b[t, r, :]).astype(jnp.bfloat16)
        over_rows(step)
        zc[t].start()

    stage_core(rs_order[0])
    for i, t in enumerate(rs_order):
        stage_first(t)
        if i + 1 < nz:
            stage_core(rs_order[i + 1])
        else:
            for copy in small:
                copy.wait()
            st[1:2, :] = jnp.broadcast_to(jnp.sum(row_state[...], axis=1, keepdims=True), (1, columns))
            early = [k for k in rs_order[:-2] if k]
            for k in early:
                zc[k].wait_recv()

            def gathered(r):
                summed[r, :] = add(lg[0, x, y, r, :], *[rz[k, r, :] for k in early])
            over_rows(gathered)
        stage_second(t)
    for t in rs_order[-2:]:
        if t:
            zc[t].wait_recv()
    late = [t for t in rs_order[-2:] if t]

    def final(i, carry):
        r = pl.ds(pl.multiple_of(i * TILE, TILE), TILE)
        left = add(summed[r, lo], r1a[0, 1, r, :], r2a[0, r, :], *[rz[t, r, lo] for t in late])
        right = add(summed[r, hi], r1b[0, 1, r, :], r2b[0, r, :], *[rz[t, r, hi] for t in late])
        summed[r, lo] = left
        summed[r, hi] = right
        left, right = left * left, right * right
        own[r, :] = jnp.sum(left, axis=1, keepdims=True) + jnp.sum(right, axis=1, keepdims=True)
        return (carry[0] + left, carry[1] + right)

    zero = jnp.zeros((TILE, half), f32)
    left, right = lax.fori_loop(0, tiles, final, (zero, zero))
    st[0:1, lo] = jnp.sum(left, axis=0, keepdims=True)
    st[0:1, hi] = jnp.sum(right, axis=0, keepdims=True)

    me = gx * 2 + y
    sends = []
    for k, peer in enumerate(plane):
        sends.append(rdma(st, st1.at[me], s1s.at[k], s1r.at[k], peer))
        sends[-1].start()
    st1[me] = st[...]
    for t in rs_order:
        for k in range(len(blocks)):
            core[t, k].wait_send()
        for copy in (fa[t], fb[t], ga[t], gb[t], ha[t], hb[t]):
            copy.wait_send()
        if t:
            zc[t].wait_send()
    for copy in sends:
        copy.wait_recv()
    total = st1[0]
    for k in range(1, nx * 2):
        total = total + st1[k]
    tot[...] = total
    line_sends = []
    for t in range(1, nz):
        line_sends.append(rdma(tot, st2.at[z], s2s.at[t], s2r.at[t], (gx, zof(t), y)))
        line_sends[-1].start()
    st2[z] = total
    diagonal = lax.broadcasted_iota(jnp.int32, (rows, rows), 0) == lax.broadcasted_iota(jnp.int32, (rows, rows), 1)
    state_down = jnp.sum(jnp.where(diagonal, jnp.broadcast_to(row_state[...], (rows, rows)), 0.0), axis=1, keepdims=True)
    for copy in line_sends:
        copy.wait_recv()
    total = st2[0]
    for k in range(1, nz):
        total = total + st2[k]
    column_sum = total[0:1, :]
    norm_square = jnp.sum(column_sum, axis=1, keepdims=True)
    state_sum = total[1:2, 0:1]
    clip_level = 0.5 * math.sqrt(full_width * columns)
    factor = jnp.minimum(jnp.float32(1.0), clip_level / jnp.sqrt(norm_square + 1e-06))
    square_factor = factor * factor
    column_next = beta_two * col_state[...] + (1.0 - beta_two) * (square_factor * column_sum / full_width)
    row_average = (beta_two * state_sum + (1.0 - beta_two) * (square_factor * norm_square / columns)) / full_width
    row_next = beta_two * state_down + (1.0 - beta_two) * (square_factor * own[...] / columns)
    own[...] = (step_size * factor) / jnp.sqrt(row_next / row_average)
    col_scale = 1.0 / jnp.sqrt(column_next)

    def update(r):
        new = params[r, :].astype(f32) - (summed[r, :] * own[r, :]) * col_scale
        full[x, c, z, y, r, :] = new.astype(jnp.bfloat16)
    over_rows(update)

    def same(view, ssem, rsem, peer):
        return rdma(view, view, ssem, rsem, peer)

    gz, q1a, q1b, q2a, q2b, q3a, q3b, gc = {}, {}, {}, {}, {}, {}, {}, {}
    for t in range(nz):
        u = zof(t)
        if t:
            gz[t] = rdma(full.at[x, c, z, y], full.at[x, c, z, y], gzs.at[t], gzr.at[t], (gx, u, y))
        q1a[t] = same(full.at[x, c, u, y, :, lo], q1as.at[t], q1ar.at[t], y_peer)
        q1b[t] = same(full.at[x, c, u, y, :, hi], q1bs.at[t], q1br.at[t], x_peer)
        q2a[t] = same(full.at[x, c, u, y, :, lo], q2as.at[t], q2ar.at[t], x_peer)
        q2b[t] = same(full.at[x, c, u, y, :, hi], q2bs.at[t], q2br.at[t], y_peer)
        q3a[t] = same(full.at[x, c, u, 1 - y, :, lo], q3as.at[t], q3ar.at[t], x_peer)
        q3b[t] = same(full.at[1 - x, c, u, y, :, hi], q3bs.at[t], q3br.at[t], y_peer)
        for k, (bx, by) in enumerate(blocks):
            gc[t, k] = same(full.at[bx, c, u, by], gcs.at[t, k], gcr.at[t, k], core_peer)

    def gather_own(t):
        if t:
            gz[t].wait_recv()
        for copy in (q1a[t], q1b[t], q2a[t], q2b[t]):
            copy.start()
        gc[t, 3].start()

    def gather_cross(t):
        q1a[t].wait_recv()
        q1b[t].wait_recv()
        q3a[t].start()
        q3b[t].start()

    def gather_side(t):
        q2a[t].wait_recv()
        gc[t, 1].start()
        q2b[t].wait_recv()
        gc[t, 2].start()

    def gather_far(t):
        q3a[t].wait_recv()
        q3b[t].wait_recv()
        gc[t, 0].start()

    q1a[0].start()
    q1b[0].start()
    for t in range(1, nz):
        gz[t].start()
    q2a[0].start()
    q2b[0].start()
    gc[0, 3].start()
    new_ref[...] = full[x, c, z, y]
    col_ref[...] = column_next
    row_ref[...] = jnp.sum(jnp.where(diagonal, jnp.broadcast_to(row_next, (rows, rows)), 0.0), axis=0, keepdims=True)
    gather_cross(0)
    for t in range(1, nz):
        gather_own(t)
        gather_side(t - 1)
        gather_far(t - 1)
        gather_cross(t)
    gather_side(nz - 1)
    gather_far(nz - 1)
    for copy in sends + line_sends:
        copy.wait_send()
    for t in range(nz):
        if t:
            gz[t].wait_send()
        for copy in (q1a[t], q1b[t], q2a[t], q2b[t], q3a[t], q3b[t]):
            copy.wait_send()
        for k in range(len(blocks)):
            gc[t, k].wait_send()
            gc[t, k].wait_recv()


def write_out(nz, new, row, col, full, new_out, row_out, col_out, full_out, sem):
    pairs = [(full.at[a, b, u], full_out.at[a, b, u]) for a in range(2) for b in range(2) for u in range(nz)]
    pairs += [(new, new_out), (row, row_out), (col, col_out)]
    copies = [pltpu.make_async_copy(src, dst, sem.at[k]) for k, (src, dst) in enumerate(pairs)]
    for copy in copies:
        copy.start()
    for copy in copies:
        copy.wait()


def fused(nx, nz, grad_bucket, parameters, row_state, column_state):
    _, _, full_width, columns = grad_bucket.shape
    rows = parameters.shape[1]
    half = columns // 2
    bf16, f32 = jnp.bfloat16, jnp.float32
    vmem = pl.BlockSpec(memory_space=pltpu.VMEM)
    hbm = pl.BlockSpec(memory_space=pltpu.HBM)
    dma = pltpu.SemaphoreType.DMA
    shapes = [((rows, columns), bf16), ((1, rows), f32), ((1, columns), f32), ((2, 2, nz, 2, rows, columns), bf16)]
    held = 2 * columns * (rows + full_width) + 4 * (columns + -(-rows // 128) * 128)
    results = pl.pallas_call(
        functools.partial(kernel, nx, nz),
        out_shape=tuple(pltpu.VMEM(*shape) for shape in shapes),
        in_specs=[hbm] * 4,
        out_specs=(vmem,) * 4,
        scratch_shapes=[
            pltpu.VMEM((nz, 2, 2, rows, columns), bf16),
            pltpu.VMEM((nz, 4, rows, columns), bf16),
            pltpu.VMEM((nz, 2, rows, half), bf16),
            pltpu.VMEM((nz, 2, rows, half), bf16),
            pltpu.VMEM((nz, rows, half), bf16),
            pltpu.VMEM((nz, rows, half), bf16),
            pltpu.VMEM((nz, rows, columns), bf16),
            pltpu.VMEM((rows, columns), f32),
            pltpu.VMEM((rows, 1), f32),
            pltpu.VMEM((2, columns), f32),
            pltpu.VMEM((nx * 2, 2, columns), f32),
            pltpu.VMEM((2, columns), f32),
            pltpu.VMEM((nz, 2, columns), f32),
            pltpu.VMEM((rows, columns), bf16),
            pltpu.VMEM((1, rows), f32),
            pltpu.VMEM((1, columns), f32),
        ] + [dma((nz,)), dma((3,))] + [dma((nz, 4))] * 2 + [dma((nz,))] * 14
        + [dma((nx * 2,))] * 2 + [dma((nz,))] * 16 + [dma((nz, 4))] * 2,
        compiler_params=pltpu.CompilerParams(
            collective_id=0, has_side_effects=True, vmem_limit_bytes=VMEM_BYTES - held),
    )(grad_bucket.reshape(2, 2, nz, 2, rows, columns), parameters[0], row_state, column_state)
    new, row, col, full = pl.pallas_call(
        functools.partial(write_out, nz),
        out_shape=tuple(jax.ShapeDtypeStruct(*shape) for shape in shapes),
        in_specs=[vmem] * 4,
        out_specs=(hbm,) * 4,
        scratch_shapes=[dma((4 * nz + 3,))],
        compiler_params=pltpu.CompilerParams(vmem_limit_bytes=4 * 1024 * 1024),
    )(*[pltpu.with_memory_space_constraint(result, pltpu.VMEM) for result in results])
    return (new[None], row, col, full.reshape(full_width, columns))


def solution(mesh):
    nx, nz, ny = (mesh.shape[a] for a in AXES)
    in_specs = (
        P(AXES, None, None, None),
        P(None, AXES, None),
        P(None, AXES),
        P(),
    )
    out_specs = (P(None, AXES, None), P(None, AXES), P(), P())
    fits = nx == 4 and ny == 2 and nz & (nz - 1) == 0

    def body(grad_bucket, parameters, row_state, column_state):
        if fits and grad_bucket.shape[1] == 1 and parameters.shape[1] % TILE == 0:
            return fused(nx, nz, grad_bucket, parameters, row_state, column_state)
        return shards(grad_bucket, parameters, row_state, column_state)

    return jax.shard_map(body, mesh=mesh, in_specs=in_specs, out_specs=out_specs, check_vma=False)
```

profile of v0, /device:TPU:0, one launch (start us, length us, event | category | flops | bytes accessed | tf_op | source)
XLA Modules:
  0.0 87.2 jit_solution(2719305460358889110)
XLA Ops:
  0.6 83.4 %shard_map.75 = (bf16[112,1024]{1,0:T(8,128)(2,1)S(1)}, f32[1,112]{1,0:T(1,128)S(1)}, f32[1,1024]{1,0:T(1,128)S(1)}, bf16[2,2,4,2,112,1024]{5,4,3,2,1,0:T(8,128)(2,1)S(1)}) custom-call(bf16[2,2,4,2,112,1024]{5,4,3,2,1,0:T(8,128)(2,1)} %bitcast.4, bf16[112,1024]{1,0:T(8,128)(2,1)} %bitcast.5, f32[1,112]{1,0:T(1,128)} %row_in.1, f32[1,1024]{1,0:T(1,128)} %col_in.1), custom_call_target="tpu_custom_call" | custom-call | tf_op jit(solution)/shard_map/pallas_call | solution.py:329
  84.0 3.2 %shard_map.76 = (bf16[112,1024]{1,0:T(8,128)(2,1)}, f32[1,112]{1,0:T(1,128)}, f32[1,1024]{1,0:T(1,128)}, bf16[2,2,4,2,112,1024]{5,4,3,2,1,0:T(8,128)(2,1)}) custom-call(bf16[112,1024]{1,0:T(8,128)(2,1)S(1)} %get-tuple-element.12.new, f32[1,112]{1,0:T(1,128)S(1)} %get-tuple-element.13.row, f32[1,1024]{1,0:T(1,128)S(1)} %get-tuple-element.14.col, ...), custom_call_target="tpu_custom_call" | custom-call | tf_op jit(solution)/shard_map/pallas_call | solution.py:356
where the time goes:
time: 87.4 us; the launch traced here: 87.2 us
  Pallas kernels  86.6 us (99%)
    pallas_call x1, Pallas kernels, fused(): pl.pallas_call(functools.partial(kernel, nx, nz), out_shape=tuple((pltpu....  83.4 us
    pallas_call x1, Pallas kernels, fused(): pl.pallas_call(functools.partial(write_out, nz), out_shape=tuple((jax.Sha...  3.2 us

commit v1 on v0

v1 whole, which is shorter than its diff:
```python
import functools
import math

import jax
import jax.numpy as jnp
from jax import lax
from jax.experimental import pallas as pl
from jax.experimental.pallas import tpu as pltpu
from jax.sharding import PartitionSpec as P

beta_two = 0.8
step_size = 0.5
AXES = ("gx", "gy", "gz")
TILE = 16
VMEM_BYTES = 67043328 - 131072


def shards(grad_bucket, parameters, row_state, column_state):
    local_grad = grad_bucket[0].astype(jnp.float32)
    layer_count, full_width, columns = local_grad.shape
    summed = lax.psum_scatter(local_grad, AXES, scatter_dimension=1, tiled=True)
    clip_level = 0.5 * math.sqrt(layer_count * full_width * columns)
    squares = summed * summed
    norm_square = lax.psum(jnp.sum(squares), AXES)
    factor = jnp.minimum(jnp.float32(1.0), clip_level / jnp.sqrt(norm_square + 1e-06))
    clipped = factor * summed
    clipped_square = clipped * clipped
    row_next = beta_two * row_state + (1.0 - beta_two) * jnp.mean(clipped_square, axis=2)
    column_part, row_total = lax.psum((jnp.sum(clipped_square, axis=1), jnp.sum(row_next, axis=1)), AXES)
    column_next = beta_two * column_state + (1.0 - beta_two) * column_part / full_width
    row_average = row_total / full_width
    second = row_next[:, :, None] * column_next[:, None, :] / row_average[:, None, None]
    update = clipped / jnp.sqrt(second)
    new_parameters = (parameters.astype(jnp.float32) - step_size * update).astype(jnp.bfloat16)
    first_layer = lax.all_gather(new_parameters[0], AXES, axis=0, tiled=True)
    return (new_parameters, row_next, column_next, first_layer)


def flip(index, mask, size):
    out, bit = 0, 1
    while bit < size:
        out = out + bit * (((index // bit) % 2 + (mask // bit) % 2) % 2)
        bit *= 2
    return out


def kernel(nx, nz, grad, params_in, row_in, col_in, new_ref, row_ref, col_ref, full,
           lg, cr, rx, rz, rc, summed, own, st, st1, tot, st2, params, row_state, col_state,
           lsem, isem, cs, cfr, cvr, fs, fr, hr, zs, zr, ks, kr, s1s, s1r, s2s, s2r,
           gzs, gzr, qs, q1r, q2r, q3r, gks, gkr, gcs, gcr):
    gx, z, y = lax.axis_index("gx"), lax.axis_index("gy"), lax.axis_index("gz")
    x, c = gx // 2, gx % 2
    rows, columns = params.shape
    lane = columns // 8
    stat_width = st.shape[1]
    full_width = rows * 4 * nz * 2
    core_peer = (x * 2 + 1 - c, z, y)
    x_peer = ((1 - x) * 2 + c, z, y)
    y_peer = (gx, z, 1 - y)
    tiles = rows // TILE
    f32, bf16 = jnp.float32, jnp.bfloat16
    scope = jax.named_scope
    blocks = [(1 - x, 1 - y), (1 - x, y), (x, 1 - y), (x, y)]
    every, flat, line_cols = pl.ds(0, columns), pl.ds(0, 7 * lane), pl.ds(7 * lane, lane)

    def zof(t):
        return flip(z, t, nz)

    def spans(t):
        low = pl.ds(0, 4 * lane)
        high = pl.ds(4 * lane, 3 * lane if t else 4 * lane)
        return (high, low) if t % 2 else (low, high)

    def width(t):
        return flat if t else every

    at_end = (z == 0) | (z == nz - 1)
    near, middle = (gx, zof(1), y), (gx, zof(3), y)

    def rdma(src, dst, ssem, rsem, peer):
        return pltpu.make_async_remote_copy(
            src_ref=src, dst_ref=dst, send_sem=ssem, recv_sem=rsem,
            device_id=peer, device_id_type=pl.DeviceIdType.MESH)

    def take_recv(view, sem):
        rdma(view, view, sem, sem, core_peer).wait_recv()

    def take_send(view, sem):
        rdma(view, view, sem, sem, core_peer).wait_send()

    rs_order = [3, 2, 1, 0]
    first = rs_order[0]
    loads = {t: pltpu.make_async_copy(grad.at[:, c, zof(t)], lg.at[t], lsem.at[t]) for t in rs_order}
    for t in rs_order:
        loads[t].start()
    small = [pltpu.make_async_copy(src, dst, isem.at[k]) for k, (src, dst) in enumerate(
        [(params_in, params), (row_in, row_state), (col_in, col_state)])]
    for copy in small:
        copy.start()

    barrier = pltpu.get_barrier_semaphore()
    plane = [((gx + a) % nx, z, (y + b) % 2) for a in range(nx) for b in range(2) if (a, b) != (0, 0)]
    line = [(gx, zof(t), y) for t in range(1, nz)]
    for peer in line + plane:
        pl.semaphore_signal(barrier, inc=1, device_id=peer, device_id_type=pl.DeviceIdType.MESH)
    with scope("barrier"):
        pl.semaphore_wait(barrier, len(plane) + len(line))

    for k, (bx, by) in enumerate(blocks):
        rdma(grad.at[bx, 1 - c, zof(first), by], cr.at[first, bx, by], cs, cfr.at[k], core_peer).start()
    for t in rs_order[1:]:
        rdma(grad.at[:, 1 - c, zof(t)], cr.at[t], cs, cvr.at[t], core_peer).start()

    def add(*terms):
        total = terms[0].astype(f32)
        for term in terms[1:]:
            total = total + term.astype(f32)
        return total

    def over_rows(step):
        @pl.loop(0, tiles, unroll=True)
        def _(i):
            step(pl.ds(pl.multiple_of(i * TILE, TILE), TILE))

    def pair_sum(t, bx, by):
        def step(r):
            lg[t, bx, by, r, :] = add(lg[t, bx, by, r, :], cr[t, bx, by, r, :]).astype(bf16)
        over_rows(step)

    def cross(t):
        return fs.at[1 if t else 0]

    def send_f(t):
        a, b = spans(t)
        rdma(lg.at[t, 1 - x, 1 - y, :, a], rx.at[t, 0, :, a], cross(t), fr.at[t], x_peer).start()
        rdma(lg.at[t, 1 - x, 1 - y, :, b], rx.at[t, 0, :, b], cross(t), fr.at[t], y_peer).start()

    def send_ga(t):
        a, b = spans(t)
        rdma(lg.at[t, 1 - x, y, :, a], rx.at[t, 1, :, a], cross(t), hr.at[t], x_peer).start()

    def send_gb(t):
        a, b = spans(t)
        rdma(lg.at[t, x, 1 - y, :, b], rx.at[t, 1, :, b], cross(t), hr.at[t], y_peer).start()

    def send_h(t):
        a, b = spans(t)
        rdma(lg.at[t, x, 1 - y, :, a], rx.at[t, 2, :, a], cross(t), hr.at[t], y_peer).start()
        rdma(lg.at[t, 1 - x, y, :, b], rx.at[t, 2, :, b], cross(t), hr.at[t], x_peer).start()

    def send_all(t):
        send_f(t)
        send_ga(t)
        send_gb(t)

    def send_line(t, slot, peer):
        rdma(lg.at[t, :, :, :, line_cols], rc.at[slot], ks, kr.at[slot], peer).start()

    def line_add(t, *slots):
        for bx in range(2):
            for by in range(2):
                def step(r):
                    lg[t, bx, by, r, line_cols] = add(
                        lg[t, bx, by, r, line_cols], *[rc[slot, bx, by, r, :] for slot in slots]).astype(bf16)
                over_rows(step)

    def stage_pair(t):
        with scope(f"pair{t}"):
            take_recv(cr.at[t], cvr.at[t])
            loads[t].wait()
            for bx, by in blocks:
                pair_sum(t, bx, by)

    def stage_first(t):
        a, b = spans(t)
        with scope(f"f{t}"):
            take_recv(rx.at[t, 0, :, width(t)], fr.at[t])

        def step(r):
            lg[t, x, 1 - y, r, a] = add(lg[t, x, 1 - y, r, a], rx[t, 0, r, a]).astype(bf16)
            lg[t, 1 - x, y, r, b] = add(lg[t, 1 - x, y, r, b], rx[t, 0, r, b]).astype(bf16)
        over_rows(step)
        send_h(t)

    def stage_second(t):
        with scope(f"h{t}"):
            take_recv(rx.at[t, 1:3, :, width(t)], hr.at[t])
        if t == 0:
            return

        def step(r):
            lg[t, x, y, r, flat] = add(lg[t, x, y, r, flat], rx[t, 1, r, flat], rx[t, 2, r, flat]).astype(bf16)
        over_rows(step)
        rdma(lg.at[t, x, y, :, flat], rz.at[t, :, flat], zs, zr.at[t], (gx, zof(t), y)).start()

    loads[first].wait()
    for k, (bx, by) in enumerate(blocks):
        with scope(f"core{k}"):
            take_recv(cr.at[first, bx, by], cfr.at[k])
        pair_sum(first, bx, by)
        if k == 0:
            send_f(first)
        elif k == 1:
            send_ga(first)
        elif k == 2:
            send_gb(first)
    for t in (3, 2, 1, 0):
        if t != first:
            stage_pair(t)
        if t:
            @pl.when(at_end)
            def _():
                send_line(t, t, near)
    stage_first(3)
    send_all(2)

    @pl.when(jnp.logical_not(at_end))
    def _():
        with scope("line3"):
            take_recv(rc.at[3], kr.at[3])
        line_add(2, 3)
        send_line(2, 4, middle)
        with scope("line2"):
            take_recv(rc.at[2], kr.at[2])
        line_add(3, 2)
        send_line(3, 5, middle)

    stage_second(3)

    @pl.when(jnp.logical_not(at_end))
    def _():
        with scope("line4"):
            take_recv(rc.at[4], kr.at[4])
        line_add(1, 4)
        send_line(1, 0, near)

    stage_first(2)
    send_all(1)
    stage_second(2)

    @pl.when(at_end)
    def _():
        with scope("line0"):
            take_recv(rc.at[0], kr.at[0])
        line_add(0, 0)

    @pl.when(jnp.logical_not(at_end))
    def _():
        with scope("line15"):
            take_recv(rc.at[1], kr.at[1])
            take_recv(rc.at[5], kr.at[5])
        line_add(0, 1, 5)

    stage_first(1)
    send_all(0)
    stage_second(1)
    stage_first(0)
    for copy in small:
        copy.wait()
    st[:, columns:] = jnp.broadcast_to(jnp.sum(row_state[...], axis=1, keepdims=True), (1, stat_width - columns))
    with scope("zearly"):
        for t in (3, 2):
            take_recv(rz.at[t, :, flat], zr.at[t])

    def gathered(r):
        summed[r, flat] = add(lg[0, x, y, r, flat], rz[3, r, flat], rz[2, r, flat])
        summed[r, line_cols] = lg[0, x, y, r, line_cols].astype(f32)
    over_rows(gathered)
    stage_second(0)
    with scope("zlate"):
        take_recv(rz.at[1, :, flat], zr.at[1])

    def final(i, carry):
        r = pl.ds(pl.multiple_of(i * TILE, TILE), TILE)
        left = add(summed[r, flat], rx[0, 1, r, flat], rx[0, 2, r, flat], rz[1, r, flat])
        right = add(summed[r, line_cols], rx[0, 1, r, line_cols], rx[0, 2, r, line_cols])
        summed[r, flat] = left
        summed[r, line_cols] = right
        left, right = left * left, right * right
        own[r, :] = jnp.sum(left, axis=1, keepdims=True) + jnp.sum(right, axis=1, keepdims=True)
        return (carry[0] + left, carry[1] + right)

    with scope("final"):
        left, right = lax.fori_loop(
            0, tiles, final, (jnp.zeros((TILE, 7 * lane), f32), jnp.zeros((TILE, lane), f32)), unroll=True)
        st[:, flat] = jnp.sum(left, axis=0, keepdims=True)
        st[:, line_cols] = jnp.sum(right, axis=0, keepdims=True)

    me = gx * 2 + y
    for peer in plane:
        rdma(st, st1.at[me], s1s, s1r, peer).start()
    st1[me] = st[...]
    take_send(cr, cs)
    take_send(rx.at[0], fs.at[0])
    take_send(rx.at[1:nz, :, :, flat], fs.at[1])
    take_send(rz.at[1:nz, :, flat], zs)
    take_send(rc.at[0:3], ks)
    diagonal = lax.broadcasted_iota(jnp.int32, (rows, rows), 0) == lax.broadcasted_iota(jnp.int32, (rows, rows), 1)
    state_down = jnp.sum(jnp.where(diagonal, jnp.broadcast_to(row_state[...], (rows, rows)), 0.0), axis=1, keepdims=True)
    with scope("stat1"):
        take_recv(st1.at[0:nx * 2 - 1], s1r)
    total = st1[0]
    for k in range(1, nx * 2):
        total = total + st1[k]
    tot[...] = total
    for t in range(1, nz):
        rdma(tot, st2.at[z], s2s, s2r, (gx, zof(t), y)).start()
    st2[z] = total
    with scope("stat2"):
        take_recv(st2.at[0:nz - 1], s2r)
    total = st2[0]
    for k in range(1, nz):
        total = total + st2[k]
    column_sum = total[:, 0:columns]
    norm_square = jnp.sum(column_sum, axis=1, keepdims=True)
    state_sum = total[:, columns:columns + 1]
    clip_level = 0.5 * math.sqrt(full_width * columns)
    factor = jnp.minimum(jnp.float32(1.0), clip_level / jnp.sqrt(norm_square + 1e-06))
    square_factor = factor * factor
    column_next = beta_two * col_state[...] + (1.0 - beta_two) * (square_factor * column_sum / full_width)
    row_average = (beta_two * state_sum + (1.0 - beta_two) * (square_factor * norm_square / columns)) / full_width
    row_next = beta_two * state_down + (1.0 - beta_two) * (square_factor * own[...] / columns)
    own[...] = (step_size * factor) / jnp.sqrt(row_next / row_average)
    col_scale = 1.0 / jnp.sqrt(column_next)

    def update(r):
        new = params[r, :].astype(f32) - (summed[r, :] * own[r, :]) * col_scale
        full[x, c, z, y, r, :] = new.astype(bf16)
    with scope("update"):
        over_rows(update)

    def same(view, ssem, rsem, peer):
        rdma(view, view, ssem, rsem, peer).start()

    def moves(t):
        return qs.at[1 if t else 0]

    def pass_core(view):
        same(view, gcs, gcr, core_peer)

    def send_q1(t):
        u, (a, b) = zof(t), spans(t)
        same(full.at[x, c, u, y, :, a], moves(t), q1r.at[t], y_peer)
        same(full.at[x, c, u, y, :, b], moves(t), q1r.at[t], x_peer)

    def send_q2(t):
        u, (a, b) = zof(t), spans(t)
        same(full.at[x, c, u, y, :, a], moves(t), q2r.at[t], x_peer)
        same(full.at[x, c, u, y, :, b], moves(t), q2r.at[t], y_peer)
        pass_core(full.at[x, c, u, y, :, width(t)])

    def gather_own(t):
        with scope(f"gz{t}"):
            take_recv(full.at[x, c, zof(t), y, :, flat], gzr.at[t])
        send_q1(t)
        send_q2(t)

    def gather_cross(t):
        u, (a, b) = zof(t), spans(t)
        with scope(f"q1_{t}"):
            take_recv(full.at[x, c, u, y, :, width(t)], q1r.at[t])
        same(full.at[x, c, u, 1 - y, :, a], moves(t), q3r.at[t], x_peer)
        same(full.at[1 - x, c, u, y, :, b], moves(t), q3r.at[t], y_peer)

    def gather_side(t):
        u = zof(t)
        with scope(f"q2_{t}"):
            take_recv(full.at[x, c, u, y, :, width(t)], q2r.at[t])
        pass_core(full.at[1 - x, c, u, y, :, width(t)])
        pass_core(full.at[x, c, u, 1 - y, :, width(t)])

    def gather_far(t):
        u = zof(t)
        with scope(f"q3_{t}"):
            take_recv(full.at[x, c, u, y, :, width(t)], q3r.at[t])
        pass_core(full.at[1 - x, c, u, 1 - y, :, width(t)])

    def strip(t):
        return full.at[:, c, zof(t), :, :, line_cols]

    def pass_strip(t, slot, peer):
        same(strip(t), gks, gkr.at[slot], peer)

    def take_strip(t):
        with scope(f"strip{t}"):
            take_recv(strip(t), gkr.at[t])
        pass_core(strip(t))

    inner = jnp.logical_not(at_end)
    send_q1(0)
    for t in range(1, nz):
        same(full.at[x, c, z, y, :, flat], gzs, gzr.at[t], (gx, zof(t), y))
    send_q2(0)
    new_ref[...] = full[x, c, z, y]
    col_ref[...] = column_next
    row_ref[...] = jnp.sum(jnp.where(diagonal, jnp.broadcast_to(row_next, (rows, rows)), 0.0), axis=0, keepdims=True)
    gather_cross(0)
    gather_own(1)
    gather_side(0)
    gather_far(0)
    pass_strip(0, 1, near)

    @pl.when(inner)
    def _():
        pass_strip(0, 3, middle)

    gather_cross(1)
    gather_own(2)
    gather_side(1)
    gather_far(1)
    gather_cross(2)
    gather_own(3)
    take_strip(1)

    @pl.when(inner)
    def _():
        pass_strip(1, 2, middle)

    gather_side(2)
    gather_far(2)

    @pl.when(inner)
    def _():
        take_strip(3)
        pass_strip(3, 2, near)

    gather_cross(3)

    @pl.when(inner)
    def _():
        take_strip(2)
        pass_strip(2, 3, near)

    gather_side(3)

    @pl.when(at_end)
    def _():
        take_strip(2)

    gather_far(3)

    @pl.when(at_end)
    def _():
        take_strip(3)

    with scope("finish"):
        take_send(st1.at[0:nx * 2 - 1], s1s)
        take_send(st2.at[0:nz - 1], s2s)
        take_send(rz.at[1:nz, :, flat], gzs)
        take_send(rx.at[0], qs.at[0])
        take_send(rx.at[1:nz, :, :, flat], qs.at[1])

        @pl.when(at_end)
        def _():
            take_send(rc.at[0], gks)

        @pl.when(inner)
        def _():
            take_send(rc.at[0:5], gks)

        take_send(full.at[:, c], gcs)
        take_recv(full.at[:, c], gcr)


def write_out(nz, new, row, col, full, new_out, row_out, col_out, full_out, sem):
    pieces = [(full.at[a, b, u], full_out.at[a, b, u]) for a in range(2) for b in range(2) for u in range(nz)]
    copies = [pltpu.make_async_copy(src, dst, sem.at[0]) for src, dst in pieces]
    small = [pltpu.make_async_copy(src, dst, sem.at[k + 1])
             for k, (src, dst) in enumerate([(new, new_out), (row, row_out), (col, col_out)])]
    for copy in copies + small:
        copy.start()
    for copy in small:
        copy.wait()
    pltpu.make_async_copy(full, full_out, sem.at[0]).wait()


def fused(nx, nz, grad_bucket, parameters, row_state, column_state):
    _, _, full_width, columns = grad_bucket.shape
    rows = parameters.shape[1]
    lane = columns // 8
    bf16, f32 = jnp.bfloat16, jnp.float32
    vmem = pl.BlockSpec(memory_space=pltpu.VMEM)
    hbm = pl.BlockSpec(memory_space=pltpu.HBM)
    dma = pltpu.SemaphoreType.DMA
    one = dma(())
    shapes = [((rows, columns), bf16), ((1, rows), f32), ((1, columns), f32), ((2, 2, nz, 2, rows, columns), bf16)]
    held = 2 * columns * (rows + full_width) + 4 * (columns + -(-rows // 128) * 128)
    stat = columns + 128
    results = pl.pallas_call(
        functools.partial(kernel, nx, nz),
        out_shape=tuple(pltpu.VMEM(*shape) for shape in shapes),
        in_specs=[hbm] * 4,
        out_specs=(vmem,) * 4,
        scratch_shapes=[
            pltpu.VMEM((nz, 2, 2, rows, columns), bf16),
            pltpu.VMEM((nz, 2, 2, rows, columns), bf16),
            pltpu.VMEM((nz, 3, rows, columns), bf16),
            pltpu.VMEM((nz, rows, columns), bf16),
            pltpu.VMEM((6, 2, 2, rows, lane), bf16),
            pltpu.VMEM((rows, columns), f32),
            pltpu.VMEM((rows, 1), f32),
            pltpu.VMEM((1, stat), f32),
            pltpu.VMEM((nx * 2, 1, stat), f32),
            pltpu.VMEM((1, stat), f32),
            pltpu.VMEM((nz, 1, stat), f32),
            pltpu.VMEM((rows, columns), bf16),
            pltpu.VMEM((1, rows), f32),
            pltpu.VMEM((1, columns), f32),
            dma((nz,)), dma((3,)), one, dma((4,)), dma((nz,)), dma((2,)), dma((nz,)), dma((nz,)),
            one, dma((nz,)), one, dma((6,)), one, one, one, one,
            one, dma((nz,)), dma((2,)), dma((nz,)), dma((nz,)), dma((nz,)), one, dma((nz,)), one, one,
        ],
        compiler_params=pltpu.CompilerParams(
            collective_id=0, has_side_effects=True, vmem_limit_bytes=VMEM_BYTES - held),
    )(grad_bucket.reshape(2, 2, nz, 2, rows, columns), parameters[0], row_state, column_state)
    new, row, col, full = pl.pallas_call(
        functools.partial(write_out, nz),
        out_shape=tuple(jax.ShapeDtypeStruct(*shape) for shape in shapes),
        in_specs=[vmem] * 4,
        out_specs=(hbm,) * 4,
        scratch_shapes=[dma((4,))],
        compiler_params=pltpu.CompilerParams(vmem_limit_bytes=4 * 1024 * 1024),
    )(*[pltpu.with_memory_space_constraint(result, pltpu.VMEM) for result in results])
    return (new[None], row, col, full.reshape(full_width, columns))


def solution(mesh):
    nx, nz, ny = (mesh.shape[a] for a in AXES)
    in_specs = (
        P(AXES, None, None, None),
        P(None, AXES, None),
        P(None, AXES),
        P(),
    )
    out_specs = (P(None, AXES, None), P(None, AXES), P(), P())
    fits = nx == 4 and ny == 2 and nz == 4

    def body(grad_bucket, parameters, row_state, column_state):
        if fits and grad_bucket.shape[1] == 1 and parameters.shape[1] % TILE == 0 and grad_bucket.shape[3] % 1024 == 0:
            return fused(nx, nz, grad_bucket, parameters, row_state, column_state)
        return shards(grad_bucket, parameters, row_state, column_state)

    return jax.shard_map(body, mesh=mesh, in_specs=in_specs, out_specs=out_specs, check_vma=False)
```

time: 87.4 us -> 83.8 us (0.959)
  Pallas kernels: 86.6 us -> 83 us
    pallas_call x1, Pallas kernels: 83.4 us -> 79.9 us  [fused(): pl.pallas_call(functools.partial(kernel, nx, nz), out_shape=tuple((pltpu....]
where the time goes in v1:
time: 83.8 us; the launch traced here: 83.6 us
  Pallas kernels  83 us (99%)
    pallas_call x1, Pallas kernels, fused(): pl.pallas_call(functools.partial(kernel, nx, nz), out_shape=tuple((pltpu....  79.9 us
    pallas_call x1, Pallas kernels, fused(): pl.pallas_call(functools.partial(write_out, nz), out_shape=tuple((jax.Sha...  3.06 us

profile of v1, /device:TPU:0, one launch (start us, length us, event | category | flops | bytes accessed | tf_op | source)
XLA Modules:
  0.0 83.6 jit_solution(8257528619619421224)
XLA Ops:
  0.6 79.9 %shard_map.75 = (bf16[112,1024]{1,0:T(8,128)(2,1)S(1)}, f32[1,112]{1,0:T(1,128)S(1)}, f32[1,1024]{1,0:T(1,128)S(1)}, bf16[2,2,4,2,112,1024]{5,4,3,2,1,0:T(8,128)(2,1)S(1)}) custom-call(bf16[2,2,4,2,112,1024]{5,4,3,2,1,0:T(8,128)(2,1)} %bitcast.4, bf16[112,1024]{1,0:T(8,128)(2,1)} %bitcast.5, f32[1,112]{1,0:T(1,128)} %row_in.1, f32[1,1024]{1,0:T(1,128)} %col_in.1), custom_call_target="tpu_custom_call" | custom-call | tf_op jit(solution)/shard_map/pallas_call | solution.py:489
  80.6 3.1 %shard_map.76 = (bf16[112,1024]{1,0:T(8,128)(2,1)}, f32[1,112]{1,0:T(1,128)}, f32[1,1024]{1,0:T(1,128)}, bf16[2,2,4,2,112,1024]{5,4,3,2,1,0:T(8,128)(2,1)}) custom-call(bf16[112,1024]{1,0:T(8,128)(2,1)S(1)} %get-tuple-element.12.new, f32[1,112]{1,0:T(1,128)S(1)} %get-tuple-element.13.row, f32[1,1024]{1,0:T(1,128)S(1)} %get-tuple-element.14.col, ...), custom_call_target="tpu_custom_call" | custom-call | tf_op jit(solution)/shard_map/pallas_call | solution.py:516

commit v2 on v1

--- a/solution.py
+++ b/solution.py
@@ -74,8 +74,15 @@
     def width(t):
         return flat if t else every
 
-    at_end = (z == 0) | (z == nz - 1)
+    inside = (z + z // 2) % 2
     near, middle = (gx, zof(1), y), (gx, zof(3), y)
+    origin = [z, zof(1), flip(z, 2 + inside, nz), flip(z, 3 - inside, nz)]
+
+    def on_end(step):
+        pl.when(inside == 0)(step)
+
+    def on_inner(step):
+        pl.when(inside == 1)(step)
 
     def rdma(src, dst, ssem, rsem, peer):
         return pltpu.make_async_remote_copy(
@@ -182,16 +189,22 @@
         over_rows(step)
         send_h(t)
 
+    def send_far(t, slot, peer):
+        rdma(lg.at[t, x, y, :, flat], rz.at[slot, :, flat], zs, zr.at[slot], peer).start()
+
+    def take_far(slot):
+        with scope(f"far{slot}"):
+            take_recv(rz.at[slot, :, flat], zr.at[slot])
+
+    def second_add(t, *slots):
+        def step(r):
+            lg[t, x, y, r, flat] = add(lg[t, x, y, r, flat], rx[t, 1, r, flat], rx[t, 2, r, flat],
+                                       *[rz[slot, r, flat] for slot in slots]).astype(bf16)
+        over_rows(step)
+
     def stage_second(t):
         with scope(f"h{t}"):
             take_recv(rx.at[t, 1:3, :, width(t)], hr.at[t])
-        if t == 0:
-            return
-
-        def step(r):
-            lg[t, x, y, r, flat] = add(lg[t, x, y, r, flat], rx[t, 1, r, flat], rx[t, 2, r, flat]).astype(bf16)
-        over_rows(step)
-        rdma(lg.at[t, x, y, :, flat], rz.at[t, :, flat], zs, zr.at[t], (gx, zof(t), y)).start()
 
     loads[first].wait()
     for k, (bx, by) in enumerate(blocks):
@@ -204,17 +217,20 @@
             send_ga(first)
         elif k == 2:
             send_gb(first)
-    for t in (3, 2, 1, 0):
-        if t != first:
-            stage_pair(t)
-        if t:
-            @pl.when(at_end)
-            def _():
-                send_line(t, t, near)
+    on_end(lambda: send_line(3, 3, near))
+    stage_pair(2)
+    on_end(lambda: send_line(2, 2, near))
     stage_first(3)
     send_all(2)
-
-    @pl.when(jnp.logical_not(at_end))
+    stage_pair(1)
+    on_end(lambda: send_line(1, 1, near))
+    stage_pair(0)
+
+    @on_end
+    def _():
+        rz[5] = jnp.zeros((rows, columns), bf16)
+
+    @on_inner
     def _():
         with scope("line3"):
             take_recv(rc.at[3], kr.at[3])
@@ -226,8 +242,10 @@
         send_line(3, 5, middle)
 
     stage_second(3)
-
-    @pl.when(jnp.logical_not(at_end))
+    second_add(3)
+    on_end(lambda: send_far(3, 3, near))
+
+    @on_inner
     def _():
         with scope("line4"):
             take_recv(rc.at[4], kr.at[4])
@@ -238,14 +256,19 @@
     send_all(1)
     stage_second(2)
 
-    @pl.when(at_end)
-    def _():
+    @on_end
+    def _():
+        second_add(2)
+        send_far(2, 2, near)
         with scope("line0"):
             take_recv(rc.at[0], kr.at[0])
         line_add(0, 0)
 
-    @pl.when(jnp.logical_not(at_end))
-    def _():
+    @on_inner
+    def _():
+        take_far(3)
+        second_add(2, 3)
+        send_far(2, 4, middle)
         with scope("line15"):
             take_recv(rc.at[1], kr.at[1])
             take_recv(rc.at[5], kr.at[5])
@@ -253,27 +276,41 @@
 
     stage_first(1)
     send_all(0)
+
+    @on_inner
+    def _():
+        take_far(2)
+
+        def step(r):
+            lg[3, x, y, r, flat] = add(lg[3, x, y, r, flat], rz[2, r, flat]).astype(bf16)
+        over_rows(step)
+        send_far(3, 5, middle)
+
     stage_second(1)
+
+    @on_end
+    def _():
+        second_add(1)
+        send_far(1, 1, near)
+
+    @on_inner
+    def _():
+        take_far(4)
+        second_add(1, 4)
+        send_far(1, 1, near)
+
     stage_first(0)
     for copy in small:
         copy.wait()
     st[:, columns:] = jnp.broadcast_to(jnp.sum(row_state[...], axis=1, keepdims=True), (1, stat_width - columns))
-    with scope("zearly"):
-        for t in (3, 2):
-            take_recv(rz.at[t, :, flat], zr.at[t])
-
-    def gathered(r):
-        summed[r, flat] = add(lg[0, x, y, r, flat], rz[3, r, flat], rz[2, r, flat])
-        summed[r, line_cols] = lg[0, x, y, r, line_cols].astype(f32)
-    over_rows(gathered)
     stage_second(0)
-    with scope("zlate"):
-        take_recv(rz.at[1, :, flat], zr.at[1])
+    take_far(1)
+    on_inner(lambda: take_far(5))
 
     def final(i, carry):
         r = pl.ds(pl.multiple_of(i * TILE, TILE), TILE)
-        left = add(summed[r, flat], rx[0, 1, r, flat], rx[0, 2, r, flat], rz[1, r, flat])
-        right = add(summed[r, line_cols], rx[0, 1, r, line_cols], rx[0, 2, r, line_cols])
+        left = add(lg[0, x, y, r, flat], rx[0, 1, r, flat], rx[0, 2, r, flat], rz[1, r, flat], rz[5, r, flat])
+        right = add(lg[0, x, y, r, line_cols], rx[0, 1, r, line_cols], rx[0, 2, r, line_cols])
         summed[r, flat] = left
         summed[r, line_cols] = right
         left, right = left * left, right * right
@@ -293,7 +330,7 @@
     take_send(cr, cs)
     take_send(rx.at[0], fs.at[0])
     take_send(rx.at[1:nz, :, :, flat], fs.at[1])
-    take_send(rz.at[1:nz, :, flat], zs)
+    take_send(rz.at[1:4, :, flat], zs)
     take_send(rc.at[0:3], ks)
     diagonal = lax.broadcasted_iota(jnp.int32, (rows, rows), 0) == lax.broadcasted_iota(jnp.int32, (rows, rows), 1)
     state_down = jnp.sum(jnp.where(diagonal, jnp.broadcast_to(row_state[...], (rows, rows)), 0.0), axis=1, keepdims=True)
@@ -339,44 +376,49 @@
         same(view, gcs, gcr, core_peer)
 
     def send_q1(t):
-        u, (a, b) = zof(t), spans(t)
+        u, (a, b) = origin[t], spans(t)
         same(full.at[x, c, u, y, :, a], moves(t), q1r.at[t], y_peer)
         same(full.at[x, c, u, y, :, b], moves(t), q1r.at[t], x_peer)
 
     def send_q2(t):
-        u, (a, b) = zof(t), spans(t)
+        u, (a, b) = origin[t], spans(t)
         same(full.at[x, c, u, y, :, a], moves(t), q2r.at[t], x_peer)
         same(full.at[x, c, u, y, :, b], moves(t), q2r.at[t], y_peer)
         pass_core(full.at[x, c, u, y, :, width(t)])
 
-    def gather_own(t):
-        with scope(f"gz{t}"):
-            take_recv(full.at[x, c, zof(t), y, :, flat], gzr.at[t])
+    def send_own(t):
         send_q1(t)
         send_q2(t)
 
+    def pass_far(t, slot, peer):
+        same(full.at[x, c, origin[t], y, :, flat], gzs, gzr.at[slot], peer)
+
+    def take_z(t):
+        with scope(f"gz{t}"):
+            take_recv(full.at[x, c, origin[t], y, :, flat], gzr.at[t])
+
     def gather_cross(t):
-        u, (a, b) = zof(t), spans(t)
+        u, (a, b) = origin[t], spans(t)
         with scope(f"q1_{t}"):
             take_recv(full.at[x, c, u, y, :, width(t)], q1r.at[t])
         same(full.at[x, c, u, 1 - y, :, a], moves(t), q3r.at[t], x_peer)
         same(full.at[1 - x, c, u, y, :, b], moves(t), q3r.at[t], y_peer)
 
     def gather_side(t):
-        u = zof(t)
+        u = origin[t]
         with scope(f"q2_{t}"):
             take_recv(full.at[x, c, u, y, :, width(t)], q2r.at[t])
         pass_core(full.at[1 - x, c, u, y, :, width(t)])
         pass_core(full.at[x, c, u, 1 - y, :, width(t)])
 
     def gather_far(t):
-        u = zof(t)
+        u = origin[t]
         with scope(f"q3_{t}"):
             take_recv(full.at[x, c, u, y, :, width(t)], q3r.at[t])
         pass_core(full.at[1 - x, c, u, 1 - y, :, width(t)])
 
     def strip(t):
-        return full.at[:, c, zof(t), :, :, line_cols]
+        return full.at[:, c, origin[t], :, :, line_cols]
 
     def pass_strip(t, slot, peer):
         same(strip(t), gks, gkr.at[slot], peer)
@@ -386,76 +428,77 @@
             take_recv(strip(t), gkr.at[t])
         pass_core(strip(t))
 
-    inner = jnp.logical_not(at_end)
+    pass_far(0, 1, near)
     send_q1(0)
-    for t in range(1, nz):
-        same(full.at[x, c, z, y, :, flat], gzs, gzr.at[t], (gx, zof(t), y))
+    on_inner(lambda: pass_far(0, 2, middle))
     send_q2(0)
     new_ref[...] = full[x, c, z, y]
     col_ref[...] = column_next
     row_ref[...] = jnp.sum(jnp.where(diagonal, jnp.broadcast_to(row_next, (rows, rows)), 0.0), axis=0, keepdims=True)
     gather_cross(0)
-    gather_own(1)
+    take_z(1)
+    on_inner(lambda: pass_far(1, 3, middle))
+    send_own(1)
+
+    @on_inner
+    def _():
+        take_z(2)
+        pass_far(2, 2, near)
+
     gather_side(0)
     gather_far(0)
     pass_strip(0, 1, near)
-
-    @pl.when(inner)
-    def _():
-        pass_strip(0, 3, middle)
-
+    on_inner(lambda: pass_strip(0, 2, middle))
     gather_cross(1)
-    gather_own(2)
+    on_end(lambda: take_z(2))
+    send_own(2)
+
+    @on_inner
+    def _():
+        take_z(3)
+        pass_far(3, 3, near)
+
     gather_side(1)
     gather_far(1)
+    take_strip(1)
+    on_inner(lambda: pass_strip(1, 3, middle))
     gather_cross(2)
-    gather_own(3)
-    take_strip(1)
-
-    @pl.when(inner)
-    def _():
-        pass_strip(1, 2, middle)
+    on_end(lambda: take_z(3))
+    send_own(3)
+
+    @on_inner
+    def _():
+        take_strip(2)
+        pass_strip(2, 2, near)
 
     gather_side(2)
     gather_far(2)
 
-    @pl.when(inner)
+    @on_inner
     def _():
         take_strip(3)
-        pass_strip(3, 2, near)
-
+        pass_strip(3, 3, near)
+
+    on_end(lambda: take_strip(2))
     gather_cross(3)
-
-    @pl.when(inner)
-    def _():
-        take_strip(2)
-        pass_strip(2, 3, near)
-
     gather_side(3)
-
-    @pl.when(at_end)
-    def _():
-        take_strip(2)
-
+    on_end(lambda: take_strip(3))
     gather_far(3)
-
-    @pl.when(at_end)
-    def _():
-        take_strip(3)
 
     with scope("finish"):
         take_send(st1.at[0:nx * 2 - 1], s1s)
         take_send(st2.at[0:nz - 1], s2s)
-        take_send(rz.at[1:nz, :, flat], gzs)
         take_send(rx.at[0], qs.at[0])
         take_send(rx.at[1:nz, :, :, flat], qs.at[1])
 
-        @pl.when(at_end)
+        @on_end
         def _():
+            take_send(rz.at[1, :, flat], gzs)
             take_send(rc.at[0], gks)
 
-        @pl.when(inner)
+        @on_inner
         def _():
+            take_send(rz.at[1:6, :, flat], gzs)
             take_send(rc.at[0:5], gks)
 
         take_send(full.at[:, c], gcs)
@@ -495,7 +538,7 @@
             pltpu.VMEM((nz, 2, 2, rows, columns), bf16),
             pltpu.VMEM((nz, 2, 2, rows, columns), bf16),
             pltpu.VMEM((nz, 3, rows, columns), bf16),
-            pltpu.VMEM((nz, rows, columns), bf16),
+            pltpu.VMEM((6, rows, columns), bf16),
             pltpu.VMEM((6, 2, 2, rows, lane), bf16),
             pltpu.VMEM((rows, columns), f32),
             pltpu.VMEM((rows, 1), f32),
@@ -507,7 +550,7 @@
             pltpu.VMEM((1, rows), f32),
             pltpu.VMEM((1, columns), f32),
             dma((nz,)), dma((3,)), one, dma((4,)), dma((nz,)), dma((2,)), dma((nz,)), dma((nz,)),
-            one, dma((nz,)), one, dma((6,)), one, one, one, one,
+            one, dma((6,)), one, dma((6,)), one, one, one, one,
             one, dma((nz,)), dma((2,)), dma((nz,)), dma((nz,)), dma((nz,)), one, dma((nz,)), one, one,
         ],
         compiler_params=pltpu.CompilerParams(

time: 83.8 us -> 80 us (0.955)
  Pallas kernels: 83 us -> 79.2 us
    pallas_call x1, Pallas kernels: 79.9 us -> 76.1 us  [fused(): pl.pallas_call(functools.partial(kernel, nx, nz), out_shape=tuple((pltpu....]
where the time goes in v2:
time: 80 us; the launch traced here: 79.9 us
  Pallas kernels  79.2 us (99%)
    pallas_call x1, Pallas kernels, fused(): pl.pallas_call(functools.partial(kernel, nx, nz), out_shape=tuple((pltpu....  76.1 us
    pallas_call x1, Pallas kernels, fused(): pl.pallas_call(functools.partial(write_out, nz), out_shape=tuple((jax.Sha...  3.06 us

profile of v2, /device:TPU:0, one launch (start us, length us, event | category | flops | bytes accessed | tf_op | source)
XLA Modules:
  0.0 79.9 jit_solution(11623177821232606557)
XLA Ops:
  0.6 76.1 %shard_map.75 = (bf16[112,1024]{1,0:T(8,128)(2,1)S(1)}, f32[1,112]{1,0:T(1,128)S(1)}, f32[1,1024]{1,0:T(1,128)S(1)}, bf16[2,2,4,2,112,1024]{5,4,3,2,1,0:T(8,128)(2,1)S(1)}) custom-call(bf16[2,2,4,2,112,1024]{5,4,3,2,1,0:T(8,128)(2,1)} %bitcast.4, bf16[112,1024]{1,0:T(8,128)(2,1)} %bitcast.5, f32[1,112]{1,0:T(1,128)} %row_in.1, f32[1,1024]{1,0:T(1,128)} %col_in.1), custom_call_target="tpu_custom_call" | custom-call | tf_op jit(solution)/shard_map/pallas_call | solution.py:532
  76.8 3.1 %shard_map.76 = (bf16[112,1024]{1,0:T(8,128)(2,1)}, f32[1,112]{1,0:T(1,128)}, f32[1,1024]{1,0:T(1,128)}, bf16[2,2,4,2,112,1024]{5,4,3,2,1,0:T(8,128)(2,1)}) custom-call(bf16[112,1024]{1,0:T(8,128)(2,1)S(1)} %get-tuple-element.12.new, f32[1,112]{1,0:T(1,128)S(1)} %get-tuple-element.13.row, f32[1,1024]{1,0:T(1,128)S(1)} %get-tuple-element.14.col, ...), custom_call_target="tpu_custom_call" | custom-call | tf_op jit(solution)/shard_map/pallas_call | solution.py:559

commit v3 on v2

v3 whole, which is shorter than its diff:
```python
import functools
import math

import jax
import jax.numpy as jnp
from jax import lax
from jax.experimental import pallas as pl
from jax.experimental.pallas import tpu as pltpu
from jax.sharding import PartitionSpec as P

beta_two = 0.8
step_size = 0.5
AXES = ("gx", "gy", "gz")
TILE = 16
VMEM_BYTES = 67043328 - 131072


def shards(grad_bucket, parameters, row_state, column_state):
    local_grad = grad_bucket[0].astype(jnp.float32)
    layer_count, full_width, columns = local_grad.shape
    summed = lax.psum_scatter(local_grad, AXES, scatter_dimension=1, tiled=True)
    clip_level = 0.5 * math.sqrt(layer_count * full_width * columns)
    squares = summed * summed
    norm_square = lax.psum(jnp.sum(squares), AXES)
    factor = jnp.minimum(jnp.float32(1.0), clip_level / jnp.sqrt(norm_square + 1e-06))
    clipped = factor * summed
    clipped_square = clipped * clipped
    row_next = beta_two * row_state + (1.0 - beta_two) * jnp.mean(clipped_square, axis=2)
    column_part, row_total = lax.psum((jnp.sum(clipped_square, axis=1), jnp.sum(row_next, axis=1)), AXES)
    column_next = beta_two * column_state + (1.0 - beta_two) * column_part / full_width
    row_average = row_total / full_width
    second = row_next[:, :, None] * column_next[:, None, :] / row_average[:, None, None]
    update = clipped / jnp.sqrt(second)
    new_parameters = (parameters.astype(jnp.float32) - step_size * update).astype(jnp.bfloat16)
    first_layer = lax.all_gather(new_parameters[0], AXES, axis=0, tiled=True)
    return (new_parameters, row_next, column_next, first_layer)


def flip(index, mask, size):
    out, bit = 0, 1
    while bit < size:
        out = out + bit * (((index // bit) % 2 + (mask // bit) % 2) % 2)
        bit *= 2
    return out


def kernel(nx, nz, grad, params_in, row_in, col_in, new_ref, row_ref, col_ref, full,
           lg, cr, rx, rz, rc, unit, summed, own, st, st1, tot, st2, params, row_state, col_state,
           lsem, isem, cs, cfr, cvr, fs, fr, hr, zs, zr, ks, kr, s1s, s1r, s2s, s2r,
           gzs, gzr, qs, q1r, q2r, q3r, gks, gkr, gcs, gcr):
    gx, z, y = lax.axis_index("gx"), lax.axis_index("gy"), lax.axis_index("gz")
    x, c = gx // 2, gx % 2
    rows, columns = params.shape
    lane = columns // 8
    stat_width = st.shape[1]
    full_width = rows * 4 * nz * 2
    core_peer = (x * 2 + 1 - c, z, y)
    x_peer = ((1 - x) * 2 + c, z, y)
    y_peer = (gx, z, 1 - y)
    tiles = rows // TILE
    f32, bf16 = jnp.float32, jnp.bfloat16
    scope = jax.named_scope
    blocks = [(1 - x, 1 - y), (1 - x, y), (x, 1 - y), (x, y)]

    cut_row = (tiles * 4 + 3) // 7
    parts = [(0, cut_row, 0, 6), (cut_row, tiles, 0, 7)]
    strips = [(0, cut_row, 6, 8), (cut_row, tiles, 7, 8)]
    halves = [(0, tiles, 0, 4), (0, tiles, 4, 8)]

    def area(regions):
        return sum((b - a) * (e - d) for a, b, d, e in regions)

    def at(region, shift=0):
        a, b, d, e = region
        return pl.ds(a * TILE, (b - a) * TILE), pl.ds((d - shift) * lane, (e - d) * lane)

    def spans(t):
        return halves if t == 0 else parts[::-1] if t % 2 else parts

    def zof(t):
        return flip(z, t, nz)

    inside = (z + z // 2) % 2
    near, middle = (gx, zof(1), y), (gx, zof(3), y)
    origin = [z, zof(1), flip(z, 2 + inside, nz), flip(z, 3 - inside, nz)]

    def on_end(step):
        pl.when(inside == 0)(step)

    def on_inner(step):
        pl.when(inside == 1)(step)

    def rdma(src, dst, ssem, rsem, peer):
        return pltpu.make_async_remote_copy(
            src_ref=src, dst_ref=dst, send_sem=ssem, recv_sem=rsem,
            device_id=peer, device_id_type=pl.DeviceIdType.MESH)

    def take_recv(view, sem):
        rdma(view, view, sem, sem, core_peer).wait_recv()

    def take_send(view, sem):
        rdma(view, view, sem, sem, core_peer).wait_send()

    def some(count):
        return unit.at[pl.ds(0, count)]

    first = 3
    loads = {t: pltpu.make_async_copy(grad.at[:, c, zof(t)], lg.at[t], lsem.at[t]) for t in (3, 2, 1, 0)}
    for t in loads:
        loads[t].start()
    small = [pltpu.make_async_copy(src, dst, isem.at[k]) for k, (src, dst) in enumerate(
        [(params_in, params), (row_in, row_state), (col_in, col_state)])]
    for copy in small:
        copy.start()

    barrier = pltpu.get_barrier_semaphore()
    plane = [((gx + a) % nx, z, (y + b) % 2) for a in range(nx) for b in range(2) if (a, b) != (0, 0)]
    line = [(gx, zof(t), y) for t in range(1, nz)]
    for peer in line + plane:
        pl.semaphore_signal(barrier, inc=1, device_id=peer, device_id_type=pl.DeviceIdType.MESH)
    with scope("barrier"):
        pl.semaphore_wait(barrier, len(plane) + len(line))

    for k, (bx, by) in enumerate(blocks):
        rdma(grad.at[bx, 1 - c, zof(first), by], cr.at[first, bx, by], cs, cfr.at[k], core_peer).start()
    for t in (2, 1, 0):
        rdma(grad.at[:, 1 - c, zof(t)], cr.at[t], cs, cvr.at[t], core_peer).start()

    def add(*terms):
        total = terms[0].astype(f32)
        for term in terms[1:]:
            total = total + term.astype(f32)
        return total

    def over(region, step, shift=0):
        a, b, d, e = region

        @pl.loop(a, b, unroll=True)
        def _(i):
            step(pl.ds(pl.multiple_of(i * TILE, TILE), TILE), pl.ds(d * lane, (e - d) * lane),
                 pl.ds((d - shift) * lane, (e - d) * lane))

    whole = (0, tiles, 0, 8)

    def pair_sum(t, bx, by):
        def step(r, l, _):
            lg[t, bx, by, r, l] = add(lg[t, bx, by, r, l], cr[t, bx, by, r, l]).astype(bf16)
        over(whole, step)

    def cross(t):
        return fs.at[1 if t else 0]

    def send(t, bx, by, slot, region, sem, peer):
        r, l = at(region)
        rdma(lg.at[t, bx, by, r, l], rx.at[t, slot, r, l], cross(t), sem.at[t], peer).start()

    def send_f(t):
        a, b = spans(t)
        send(t, 1 - x, 1 - y, 0, a, fr, x_peer)
        send(t, 1 - x, 1 - y, 0, b, fr, y_peer)

    def send_ga(t):
        send(t, 1 - x, y, 1, spans(t)[0], hr, x_peer)

    def send_gb(t):
        send(t, x, 1 - y, 1, spans(t)[1], hr, y_peer)

    def send_g(t):
        send_ga(t)
        send_gb(t)

    def send_strip(t, slot, peer):
        for region in strips:
            r, l = at(region)
            _, m = at(region, 6)
            rdma(lg.at[t, :, :, r, l], rc.at[slot, :, :, r, m], ks, kr.at[slot], peer).start()

    def take_strips(*slots):
        for slot in slots:
            with scope(f"line{slot}"):
                take_recv(some(4 * area(strips)), kr.at[slot])

    def strip_add(t, *slots):
        for bx in range(2):
            for by in range(2):
                def step(r, l, m):
                    lg[t, bx, by, r, l] = add(
                        lg[t, bx, by, r, l], *[rc[slot, bx, by, r, m] for slot in slots]).astype(bf16)
                for region in strips:
                    over(region, step, 6)

    def stage_pair(t):
        with scope(f"pair{t}"):
            take_recv(cr.at[t], cvr.at[t])
            loads[t].wait()
            for bx, by in blocks:
                pair_sum(t, bx, by)

    def stage_first(t):
        a, b = spans(t)
        with scope(f"f{t}"):
            take_recv(some(area(spans(t))), fr.at[t])

        def step_a(r, l, _):
            lg[t, x, 1 - y, r, l] = add(lg[t, x, 1 - y, r, l], rx[t, 0, r, l]).astype(bf16)

        def step_b(r, l, _):
            lg[t, 1 - x, y, r, l] = add(lg[t, 1 - x, y, r, l], rx[t, 0, r, l]).astype(bf16)
        over(a, step_a)
        send(t, x, 1 - y, 2, a, hr, y_peer)
        over(b, step_b)
        send(t, 1 - x, y, 2, b, hr, x_peer)

    def stage_second(t):
        with scope(f"h{t}"):
            take_recv(some(2 * area(spans(t))), hr.at[t])

    def send_far(t, slot, peer, p):
        r, l = at(parts[p])
        rdma(lg.at[t, x, y, r, l], rz.at[slot, r, l], zs, zr.at[slot, p], peer).start()

    def take_far(slot, p):
        with scope(f"far{slot}_{p}"):
            take_recv(some(area(parts[p:p + 1])), zr.at[slot, p])

    def second_add(t, p, *slots):
        def step(r, l, _):
            lg[t, x, y, r, l] = add(lg[t, x, y, r, l], rx[t, 1, r, l], rx[t, 2, r, l],
                                    *[rz[slot, r, l] for slot in slots]).astype(bf16)
        over(parts[p], step)

    loads[first].wait()
    for k, (bx, by) in enumerate(blocks):
        with scope(f"core{k}"):
            take_recv(cr.at[first, bx, by], cfr.at[k])
        pair_sum(first, bx, by)
        if k == 0:
            send_f(first)
        elif k == 1:
            send_ga(first)
        elif k == 2:
            send_gb(first)
    on_end(lambda: send_strip(3, 3, near))
    stage_pair(2)
    on_end(lambda: send_strip(2, 2, near))
    send_f(2)
    stage_first(3)
    send_g(2)
    stage_pair(1)
    on_end(lambda: send_strip(1, 1, near))
    send_f(1)
    stage_pair(0)

    @on_end
    def _():
        rz[5] = jnp.zeros((rows, columns), bf16)

    @on_inner
    def _():
        take_strips(3)
        strip_add(2, 3)
        send_strip(2, 4, middle)

    stage_first(2)
    send_g(1)

    @on_inner
    def _():
        take_strips(2)
        strip_add(3, 2)
        send_strip(3, 5, middle)

    stage_second(3)
    for p in range(2):
        second_add(3, p)
        on_end(lambda: send_far(3, 3, near, p))

    @on_inner
    def _():
        take_strips(4)
        strip_add(1, 4)
        send_strip(1, 0, near)

    stage_first(1)

    @on_end
    def _():
        take_strips(0)
        strip_add(0, 0)

    @on_inner
    def _():
        take_strips(1, 5)
        strip_add(0, 1, 5)

    send_f(0)
    send_g(0)
    stage_second(2)

    @on_end
    def _():
        for p in range(2):
            second_add(2, p)
            send_far(2, 2, near, p)

    @on_inner
    def _():
        for p in range(2):
            take_far(3, p)
            second_add(2, p, 3)
            send_far(2, 4, middle, p)

    def pass_far_sum(p):
        take_far(2, p)

        def step(r, l, _):
            lg[3, x, y, r, l] = add(lg[3, x, y, r, l], rz[2, r, l]).astype(bf16)
        over(parts[p], step)
        send_far(3, 5, middle, p)

    on_inner(lambda: pass_far_sum(0))
    stage_second(1)

    @on_end
    def _():
        for p in range(2):
            second_add(1, p)
            send_far(1, 1, near, p)

    @on_inner
    def _():
        pass_far_sum(1)
        for p in range(2):
            take_far(4, p)
            second_add(1, p, 4)
            send_far(1, 1, near, p)

    stage_first(0)
    for copy in small:
        copy.wait()
    st[:, columns:] = jnp.broadcast_to(jnp.sum(row_state[...], axis=1, keepdims=True), (1, stat_width - columns))
    stage_second(0)
    for p in range(2):
        take_far(1, p)

    @on_inner
    def _():
        for p in range(2):
            take_far(5, p)

    with scope("final"):
        cuts = [(0, 6), (6, 7), (7, 8)]
        sums = [None] * len(cuts)
        for i in range(tiles):
            r = pl.ds(i * TILE, TILE)
            row_sum = 0.0
            for k, (d, e) in enumerate(cuts):
                l = pl.ds(d * lane, (e - d) * lane)
                terms = [lg[0, x, y, r, l], rx[0, 1, r, l], rx[0, 2, r, l]]
                if e <= parts[0 if i < cut_row else 1][3]:
                    terms += [rz[1, r, l], rz[5, r, l]]
                value = add(*terms)
                summed[r, l] = value
                value = value * value
                row_sum = row_sum + jnp.sum(value, axis=1, keepdims=True)
                sums[k] = value if sums[k] is None else sums[k] + value
            own[r, :] = row_sum
        for (d, e), value in zip(cuts, sums):
            st[:, pl.ds(d * lane, (e - d) * lane)] = jnp.sum(value, axis=0, keepdims=True)

    me = gx * 2 + y
    for peer in plane:
        rdma(st, st1.at[me], s1s, s1r, peer).start()
    st1[me] = st[...]
    take_send(cr, cs)
    take_send(some(3 * area(halves)), fs.at[0])
    take_send(some(9 * area(parts)), fs.at[1])
    take_send(some(3 * area(parts)), zs)
    take_send(some(12 * area(strips)), ks)
    diagonal = lax.broadcasted_iota(jnp.int32, (rows, rows), 0) == lax.broadcasted_iota(jnp.int32, (rows, rows), 1)
    state_down = jnp.sum(jnp.where(diagonal, jnp.broadcast_to(row_state[...], (rows, rows)), 0.0), axis=1, keepdims=True)
    with scope("stat1"):
        take_recv(st1.at[0:nx * 2 - 1], s1r)
    total = st1[0]
    for k in range(1, nx * 2):
        total = total + st1[k]
    tot[...] = total
    for t in range(1, nz):
        rdma(tot, st2.at[z], s2s, s2r, (gx, zof(t), y)).start()
    st2[z] = total
    with scope("stat2"):
        take_recv(st2.at[0:nz - 1], s2r)
    total = st2[0]
    for k in range(1, nz):
        total = total + st2[k]
    column_sum = total[:, 0:columns]
    norm_square = jnp.sum(column_sum, axis=1, keepdims=True)
    state_sum = total[:, columns:columns + 1]
    clip_level = 0.5 * math.sqrt(full_width * columns)
    factor = jnp.minimum(jnp.float32(1.0), clip_level / jnp.sqrt(norm_square + 1e-06))
    square_factor = factor * factor
    column_next = beta_two * col_state[...] + (1.0 - beta_two) * (square_factor * column_sum / full_width)
    row_average = (beta_two * state_sum + (1.0 - beta_two) * (square_factor * norm_square / columns)) / full_width
    row_next = beta_two * state_down + (1.0 - beta_two) * (square_factor * own[...] / columns)
    own[...] = (step_size * factor) / jnp.sqrt(row_next / row_average)
    col_scale = 1.0 / jnp.sqrt(column_next)

    def update(r, l, _):
        new = params[r, l].astype(f32) - (summed[r, l] * own[r, :]) * col_scale
        full[x, c, z, y, r, l] = new.astype(bf16)
    with scope("update"):
        over(whole, update)

    def same(view, ssem, rsem, peer):
        rdma(view, view, ssem, rsem, peer).start()

    def moves(t):
        return qs.at[1 if t else 0]

    def piece(bx, u, by, region):
        r, l = at(region)
        return full.at[bx, c, u, by, r, l]

    def pass_core(t, bx, by):
        for region in parts if t else [whole]:
            same(piece(bx, origin[t], by, region), gcs, gcr, core_peer)

    def send_q1(t):
        u, (a, b) = origin[t], spans(t)
        same(piece(x, u, y, a), moves(t), q1r.at[t], y_peer)
        same(piece(x, u, y, b), moves(t), q1r.at[t], x_peer)

    def send_q2(t):
        u, (a, b) = origin[t], spans(t)
        same(piece(x, u, y, a), moves(t), q2r.at[t], x_peer)
        same(piece(x, u, y, b), moves(t), q2r.at[t], y_peer)
        pass_core(t, x, y)

    def send_own(t):
        send_q1(t)
        send_q2(t)

    def pass_far(t, slot, peer):
        for region in parts:
            same(piece(x, origin[t], y, region), gzs, gzr.at[slot], peer)

    def take_z(t):
        with scope(f"gz{t}"):
            take_recv(some(area(parts)), gzr.at[t])

    def gather_cross(t):
        u, (a, b) = origin[t], spans(t)
        with scope(f"q1_{t}"):
            take_recv(some(area(spans(t))), q1r.at[t])
        same(piece(x, u, 1 - y, a), moves(t), q3r.at[t], x_peer)
        same(piece(1 - x, u, y, b), moves(t), q3r.at[t], y_peer)

    def gather_side(t):
        with scope(f"q2_{t}"):
            take_recv(some(area(spans(t))), q2r.at[t])
        pass_core(t, 1 - x, y)
        pass_core(t, x, 1 - y)

    def gather_far(t):
        with scope(f"q3_{t}"):
            take_recv(some(area(spans(t))), q3r.at[t])
        pass_core(t, 1 - x, 1 - y)

    def each_strip(t, ssem, rsem, peer):
        for region in strips:
            r, l = at(region)
            same(full.at[:, c, origin[t], :, r, l], ssem, rsem, peer)

    def pass_strip(t, slot, peer):
        each_strip(t, gks, gkr.at[slot], peer)

    def take_strip(t):
        with scope(f"strip{t}"):
            take_recv(some(4 * area(strips)), gkr.at[t])
        each_strip(t, gcs, gcr, core_peer)

    pass_far(0, 1, near)
    send_q1(0)
    on_inner(lambda: pass_far(0, 2, middle))
    send_q2(0)
    new_ref[...] = full[x, c, z, y]
    col_ref[...] = column_next
    row_ref[...] = jnp.sum(jnp.where(diagonal, jnp.broadcast_to(row_next, (rows, rows)), 0.0), axis=0, keepdims=True)
    gather_cross(0)
    take_z(1)
    on_inner(lambda: pass_far(1, 3, middle))
    send_own(1)

    @on_inner
    def _():
        take_z(2)
        pass_far(2, 2, near)

    gather_side(0)
    gather_far(0)
    pass_strip(0, 1, near)
    on_inner(lambda: pass_strip(0, 2, middle))
    gather_cross(1)
    on_end(lambda: take_z(2))
    send_own(2)

    @on_inner
    def _():
        take_z(3)
        pass_far(3, 3, near)

    gather_side(1)
    gather_far(1)
    take_strip(1)
    on_inner(lambda: pass_strip(1, 3, middle))
    gather_cross(2)
    on_end(lambda: take_z(3))
    send_own(3)

    @on_inner
    def _():
        take_strip(2)
        pass_strip(2, 2, near)

    gather_side(2)
    gather_far(2)

    @on_inner
    def _():
        take_strip(3)
        pass_strip(3, 3, near)

    on_end(lambda: take_strip(2))
    gather_cross(3)
    gather_side(3)
    gather_far(3)
    on_end(lambda: take_strip(3))

    with scope("finish"):
        take_send(st1.at[0:nx * 2 - 1], s1s)
        take_send(st2.at[0:nz - 1], s2s)
        take_send(some(3 * area(halves)), qs.at[0])
        take_send(some(9 * area(parts)), qs.at[1])

        @on_end
        def _():
            take_send(some(area(parts)), gzs)
            take_send(some(4 * area(strips)), gks)

        @on_inner
        def _():
            take_send(some(5 * area(parts)), gzs)
            take_send(some(20 * area(strips)), gks)

        take_send(full.at[:, c], gcs)
        take_recv(full.at[:, c], gcr)


def write_out(nz, new, row, col, full, new_out, row_out, col_out, full_out, sem):
    pieces = [(full.at[a, b, u], full_out.at[a, b, u]) for a in range(2) for b in range(2) for u in range(nz)]
    copies = [pltpu.make_async_copy(src, dst, sem.at[0]) for src, dst in pieces]
    small = [pltpu.make_async_copy(src, dst, sem.at[k + 1])
             for k, (src, dst) in enumerate([(new, new_out), (row, row_out), (col, col_out)])]
    for copy in copies + small:
        copy.start()
    for copy in small:
        copy.wait()
    pltpu.make_async_copy(full, full_out, sem.at[0]).wait()


def fused(nx, nz, grad_bucket, parameters, row_state, column_state):
    _, _, full_width, columns = grad_bucket.shape
    rows = parameters.shape[1]
    lane = columns // 8
    bf16, f32 = jnp.bfloat16, jnp.float32
    vmem = pl.BlockSpec(memory_space=pltpu.VMEM)
    hbm = pl.BlockSpec(memory_space=pltpu.HBM)
    dma = pltpu.SemaphoreType.DMA
    one = dma(())
    shapes = [((rows, columns), bf16), ((1, rows), f32), ((1, columns), f32), ((2, 2, nz, 2, rows, columns), bf16)]
    held = 2 * columns * (rows + full_width) + 4 * (columns + -(-rows // 128) * 128)
    stat = columns + 128
    results = pl.pallas_call(
        functools.partial(kernel, nx, nz),
        out_shape=tuple(pltpu.VMEM(*shape) for shape in shapes),
        in_specs=[hbm] * 4,
        out_specs=(vmem,) * 4,
        scratch_shapes=[
            pltpu.VMEM((nz, 2, 2, rows, columns), bf16),
            pltpu.VMEM((nz, 2, 2, rows, columns), bf16),
            pltpu.VMEM((nz, 3, rows, columns), bf16),
            pltpu.VMEM((6, rows, columns), bf16),
            pltpu.VMEM((6, 2, 2, rows, 2 * lane), bf16),
            pltpu.VMEM((9 * 8 * (rows // TILE), TILE, lane), bf16),
            pltpu.VMEM((rows, columns), f32),
            pltpu.VMEM((rows, 1), f32),
            pltpu.VMEM((1, stat), f32),
            pltpu.VMEM((nx * 2, 1, stat), f32),
            pltpu.VMEM((1, stat), f32),
            pltpu.VMEM((nz, 1, stat), f32),
            pltpu.VMEM((rows, columns), bf16),
            pltpu.VMEM((1, rows), f32),
            pltpu.VMEM((1, columns), f32),
            dma((nz,)), dma((3,)), one, dma((4,)), dma((nz,)), dma((2,)), dma((nz,)), dma((nz,)),
            one, dma((6, 2)), one, dma((6,)), one, one, one, one,
            one, dma((nz,)), dma((2,)), dma((nz,)), dma((nz,)), dma((nz,)), one, dma((nz,)), one, one,
        ],
        compiler_params=pltpu.CompilerParams(
            collective_id=0, has_side_effects=True, vmem_limit_bytes=VMEM_BYTES - held),
    )(grad_bucket.reshape(2, 2, nz, 2, rows, columns), parameters[0], row_state, column_state)
    new, row, col, full = pl.pallas_call(
        functools.partial(write_out, nz),
        out_shape=tuple(jax.ShapeDtypeStruct(*shape) for shape in shapes),
        in_specs=[vmem] * 4,
        out_specs=(hbm,) * 4,
        scratch_shapes=[dma((4,))],
        compiler_params=pltpu.CompilerParams(vmem_limit_bytes=4 * 1024 * 1024),
    )(*[pltpu.with_memory_space_constraint(result, pltpu.VMEM) for result in results])
    return (new[None], row, col, full.reshape(full_width, columns))


def solution(mesh):
    nx, nz, ny = (mesh.shape[a] for a in AXES)
    in_specs = (
        P(AXES, None, None, None),
        P(None, AXES, None),
        P(None, AXES),
        P(),
    )
    out_specs = (P(None, AXES, None), P(None, AXES), P(), P())
    fits = nx == 4 and ny == 2 and nz == 4

    def body(grad_bucket, parameters, row_state, column_state):
        if fits and grad_bucket.shape[1] == 1 and parameters.shape[1] % TILE == 0 and parameters.shape[1] >= 2 * TILE and grad_bucket.shape[3] % 1024 == 0:
            return fused(nx, nz, grad_bucket, parameters, row_state, column_state)
        return shards(grad_bucket, parameters, row_state, column_state)

    return jax.shard_map(body, mesh=mesh, in_specs=in_specs, out_specs=out_specs, check_vma=False)
```

time: 80 us -> 78.1 us (0.976)
  Pallas kernels: 79.2 us -> 77.3 us
    pallas_call x1, Pallas kernels: 76.1 us -> 74.2 us  [fused(): pl.pallas_call(functools.partial(kernel, nx, nz), out_shape=tuple((pltpu....]
where the time goes in v3:
time: 78.1 us; the launch traced here: 77.9 us
  Pallas kernels  77.3 us (99%)
    pallas_call x1, Pallas kernels, fused(): pl.pallas_call(functools.partial(kernel, nx, nz), out_shape=tuple((pltpu....  74.2 us
    pallas_call x1, Pallas kernels, fused(): pl.pallas_call(functools.partial(write_out, nz), out_shape=tuple((jax.Sha...  3.06 us

profile of v3, /device:TPU:0, one launch (start us, length us, event | category | flops | bytes accessed | tf_op | source)
XLA Modules:
  0.0 77.9 jit_solution(17378077796477339029)
XLA Ops:
  0.6 74.2 %shard_map.75 = (bf16[112,1024]{1,0:T(8,128)(2,1)S(1)}, f32[1,112]{1,0:T(1,128)S(1)}, f32[1,1024]{1,0:T(1,128)S(1)}, bf16[2,2,4,2,112,1024]{5,4,3,2,1,0:T(8,128)(2,1)S(1)}) custom-call(bf16[2,2,4,2,112,1024]{5,4,3,2,1,0:T(8,128)(2,1)} %bitcast.4, bf16[112,1024]{1,0:T(8,128)(2,1)} %bitcast.5, f32[1,112]{1,0:T(1,128)} %row_in.1, f32[1,1024]{1,0:T(1,128)} %col_in.1), custom_call_target="tpu_custom_call" | custom-call | tf_op jit(solution)/shard_map/pallas_call | solution.py:583
  74.9 3.1 %shard_map.76 = (bf16[112,1024]{1,0:T(8,128)(2,1)}, f32[1,112]{1,0:T(1,128)}, f32[1,1024]{1,0:T(1,128)}, bf16[2,2,4,2,112,1024]{5,4,3,2,1,0:T(8,128)(2,1)}) custom-call(bf16[112,1024]{1,0:T(8,128)(2,1)S(1)} %get-tuple-element.12.new, f32[1,112]{1,0:T(1,128)S(1)} %get-tuple-element.13.row, f32[1,1024]{1,0:T(1,128)S(1)} %get-tuple-element.14.col, ...), custom_call_target="tpu_custom_call" | custom-call | tf_op jit(solution)/shard_map/pallas_call | solution.py:611

commit v4 on v3

--- a/solution.py
+++ b/solution.py
@@ -169,25 +169,36 @@
         send_ga(t)
         send_gb(t)
 
-    def send_strip(t, slot, peer):
+    side = [1 - x, x]
+
+    def send_strip(t, slot, peer, h):
         for region in strips:
             r, l = at(region)
             _, m = at(region, 6)
-            rdma(lg.at[t, :, :, r, l], rc.at[slot, :, :, r, m], ks, kr.at[slot], peer).start()
-
-    def take_strips(*slots):
+            rdma(lg.at[t, side[h], :, r, l], rc.at[slot, h, :, r, m], ks, kr.at[slot, h], peer).start()
+
+    def send_strips(t, slot, peer):
+        for h in range(2):
+            send_strip(t, slot, peer, h)
+
+    def take_strips(h, *slots):
         for slot in slots:
-            with scope(f"line{slot}"):
-                take_recv(some(4 * area(strips)), kr.at[slot])
-
-    def strip_add(t, *slots):
-        for bx in range(2):
-            for by in range(2):
-                def step(r, l, m):
-                    lg[t, bx, by, r, l] = add(
-                        lg[t, bx, by, r, l], *[rc[slot, bx, by, r, m] for slot in slots]).astype(bf16)
-                for region in strips:
-                    over(region, step, 6)
+            with scope(f"line{slot}_{h}"):
+                take_recv(some(2 * area(strips)), kr.at[slot, h])
+
+    def strip_add(t, h, *slots):
+        for by in range(2):
+            def step(r, l, m):
+                lg[t, side[h], by, r, l] = add(
+                    lg[t, side[h], by, r, l], *[rc[slot, h, by, r, m] for slot in slots]).astype(bf16)
+            for region in strips:
+                over(region, step, 6)
+
+    def relay(came, t, slot, peer):
+        for h in range(2):
+            take_strips(h, came)
+            strip_add(t, h, came)
+            send_strip(t, slot, peer, h)
 
     def stage_pair(t):
         with scope(f"pair{t}"):
@@ -238,73 +249,58 @@
             send_f(first)
         elif k == 1:
             send_ga(first)
+            on_end(lambda: send_strip(3, 3, near, 0))
         elif k == 2:
             send_gb(first)
-    on_end(lambda: send_strip(3, 3, near))
+        else:
+            on_end(lambda: send_strip(3, 3, near, 1))
     stage_pair(2)
-    on_end(lambda: send_strip(2, 2, near))
+    on_end(lambda: send_strips(2, 2, near))
     send_f(2)
     stage_first(3)
     send_g(2)
     stage_pair(1)
-    on_end(lambda: send_strip(1, 1, near))
+    on_end(lambda: send_strips(1, 1, near))
     send_f(1)
+    on_inner(lambda: relay(3, 2, 4, middle))
     stage_pair(0)
 
     @on_end
     def _():
         rz[5] = jnp.zeros((rows, columns), bf16)
-
-    @on_inner
-    def _():
-        take_strips(3)
-        strip_add(2, 3)
-        send_strip(2, 4, middle)
 
     stage_first(2)
     send_g(1)
-
-    @on_inner
-    def _():
-        take_strips(2)
-        strip_add(3, 2)
-        send_strip(3, 5, middle)
-
+    on_inner(lambda: relay(2, 3, 5, middle))
     stage_second(3)
     for p in range(2):
         second_add(3, p)
         on_end(lambda: send_far(3, 3, near, p))
-
-    @on_inner
-    def _():
-        take_strips(4)
-        strip_add(1, 4)
-        send_strip(1, 0, near)
-
+    on_inner(lambda: relay(4, 1, 0, near))
     stage_first(1)
 
     @on_end
     def _():
-        take_strips(0)
-        strip_add(0, 0)
-
-    @on_inner
-    def _():
-        take_strips(1, 5)
-        strip_add(0, 1, 5)
-
-    send_f(0)
-    send_g(0)
-    stage_second(2)
-
-    @on_end
-    def _():
+        stage_second(2)
         for p in range(2):
             second_add(2, p)
             send_far(2, 2, near, p)
-
-    @on_inner
-    def _():
+        for h in range(2):
+            take_strips(h, 0)
+            strip_add(0, h, 0)
+
+    @on_inner
+    def _():
+        for h in range(2):
+            take_strips(h, 1, 5)
+            strip_add(0, h, 1, 5)
+
+    send_f(0)
+    send_g(0)
+
+    @on_inner
+    def _():
+        stage_second(2)
         for p in range(2):
             take_far(3, p)
             second_add(2, p, 3)
@@ -318,7 +314,6 @@
         over(parts[p], step)
         send_far(3, 5, middle, p)
 
-    on_inner(lambda: pass_far_sum(0))
     stage_second(1)
 
     @on_end
@@ -327,15 +322,23 @@
             second_add(1, p)
             send_far(1, 1, near, p)
 
+    def pass_near_sum(p):
+        take_far(4, p)
+        second_add(1, p, 4)
+        send_far(1, 1, near, p)
+
+    @on_inner
+    def _():
+        pass_far_sum(0)
+        pass_near_sum(0)
+
+    stage_first(0)
+
     @on_inner
     def _():
         pass_far_sum(1)
-        for p in range(2):
-            take_far(4, p)
-            second_add(1, p, 4)
-            send_far(1, 1, near, p)
-
-    stage_first(0)
+        pass_near_sum(1)
+
     for copy in small:
         copy.wait()
     st[:, columns:] = jnp.broadcast_to(jnp.sum(row_state[...], axis=1, keepdims=True), (1, stat_width - columns))
@@ -602,7 +605,7 @@
             pltpu.VMEM((1, rows), f32),
             pltpu.VMEM((1, columns), f32),
             dma((nz,)), dma((3,)), one, dma((4,)), dma((nz,)), dma((2,)), dma((nz,)), dma((nz,)),
-            one, dma((6, 2)), one, dma((6,)), one, one, one, one,
+            one, dma((6, 2)), one, dma((6, 2)), one, one, one, one,
             one, dma((nz,)), dma((2,)), dma((nz,)), dma((nz,)), dma((nz,)), one, dma((nz,)), one, one,
         ],
         compiler_params=pltpu.CompilerParams(

time: 78.1 us -> 74.6 us (0.955)
  Pallas kernels: 77.3 us -> 73.8 us
    pallas_call x1, Pallas kernels: 74.2 us -> 70.7 us  [fused(): pl.pallas_call(functools.partial(kernel, nx, nz), out_shape=tuple((pltpu....]
where the time goes in v4:
time: 74.6 us; the launch traced here: 74.4 us
  Pallas kernels  73.8 us (99%)
    pallas_call x1, Pallas kernels, fused(): pl.pallas_call(functools.partial(kernel, nx, nz), out_shape=tuple((pltpu....  70.7 us
    pallas_call x1, Pallas kernels, fused(): pl.pallas_call(functools.partial(write_out, nz), out_shape=tuple((jax.Sha...  3.06 us

profile of v4, /device:TPU:0, one launch (start us, length us, event | category | flops | bytes accessed | tf_op | source)
XLA Modules:
  0.0 74.4 jit_solution(16507447939206484929)
XLA Ops:
  0.6 70.7 %shard_map.75 = (bf16[112,1024]{1,0:T(8,128)(2,1)S(1)}, f32[1,112]{1,0:T(1,128)S(1)}, f32[1,1024]{1,0:T(1,128)S(1)}, bf16[2,2,4,2,112,1024]{5,4,3,2,1,0:T(8,128)(2,1)S(1)}) custom-call(bf16[2,2,4,2,112,1024]{5,4,3,2,1,0:T(8,128)(2,1)} %bitcast.4, bf16[112,1024]{1,0:T(8,128)(2,1)} %bitcast.5, f32[1,112]{1,0:T(1,128)} %row_in.1, f32[1,1024]{1,0:T(1,128)} %col_in.1), custom_call_target="tpu_custom_call" | custom-call | tf_op jit(solution)/shard_map/pallas_call | solution.py:586
  71.4 3.1 %shard_map.76 = (bf16[112,1024]{1,0:T(8,128)(2,1)}, f32[1,112]{1,0:T(1,128)}, f32[1,1024]{1,0:T(1,128)}, bf16[2,2,4,2,112,1024]{5,4,3,2,1,0:T(8,128)(2,1)}) custom-call(bf16[112,1024]{1,0:T(8,128)(2,1)S(1)} %get-tuple-element.12.new, f32[1,112]{1,0:T(1,128)S(1)} %get-tuple-element.13.row, f32[1,1024]{1,0:T(1,128)S(1)} %get-tuple-element.14.col, ...), custom_call_target="tpu_custom_call" | custom-call | tf_op jit(solution)/shard_map/pallas_call | solution.py:614

commit v5 on v4

--- a/solution.py
+++ b/solution.py
@@ -45,12 +45,13 @@
 
 
 def kernel(nx, nz, grad, params_in, row_in, col_in, new_ref, row_ref, col_ref, full,
-           lg, cr, rx, rz, rc, unit, summed, own, st, st1, tot, st2, params, row_state, col_state,
+           lg, cr, rx, rz, rc, unit, sums_of, params_of, info, scale, st, st1, tot, st2, row_state, col_state,
            lsem, isem, cs, cfr, cvr, fs, fr, hr, zs, zr, ks, kr, s1s, s1r, s2s, s2r,
-           gzs, gzr, qs, q1r, q2r, q3r, gks, gkr, gcs, gcr):
+           gzs, gzr, qs, q1r, q2r, q3r, gks, gkr, gcs, gcr, ns, nr, nzs, nzr, ins, inr):
     gx, z, y = lax.axis_index("gx"), lax.axis_index("gy"), lax.axis_index("gz")
     x, c = gx // 2, gx % 2
-    rows, columns = params.shape
+    rows, columns = new_ref.shape
+    params, sums = params_of.at[0], sums_of.at[0]
     lane = columns // 8
     stat_width = st.shape[1]
     full_width = rows * 4 * nz * 2
@@ -125,6 +126,23 @@
         rdma(grad.at[bx, 1 - c, zof(first), by], cr.at[first, bx, by], cs, cfr.at[k], core_peer).start()
     for t in (2, 1, 0):
         rdma(grad.at[:, 1 - c, zof(t)], cr.at[t], cs, cvr.at[t], core_peer).start()
+
+    X, Y, NEAR, MIDDLE = 1, 2, 3, 4
+
+    def send_plane(src, dst, swap):
+        for region, (slot, peer) in zip(halves, [(X, x_peer), (Y, y_peer)] if swap else [(Y, y_peer), (X, x_peer)]):
+            r, l = at(region)
+            rdma(src.at[r, l], dst.at[slot, r, l], ns, nr.at[1 if swap else 0], peer).start()
+
+    def send_near(src, dst, slot, peer, regions):
+        for region in regions:
+            r, l = at(region)
+            rdma(src.at[r, l], dst.at[slot, r, l], nzs, nzr.at[slot - NEAR], peer).start()
+
+    @on_inner
+    def _():
+        send_near(params_in, params_of, NEAR, near, parts)
+        send_near(params_in, params_of, MIDDLE, middle, parts)
 
     def add(*terms):
         total = terms[0].astype(f32)
@@ -333,14 +351,17 @@
         pass_near_sum(0)
 
     stage_first(0)
+    for copy in small:
+        copy.wait()
+    send_plane(params, params_of, False)
 
     @on_inner
     def _():
         pass_far_sum(1)
         pass_near_sum(1)
 
-    for copy in small:
-        copy.wait()
+    on_end(lambda: send_near(params, params_of, NEAR, near, parts))
+    info[0, 0:1, :] = row_state[...]
     st[:, columns:] = jnp.broadcast_to(jnp.sum(row_state[...], axis=1, keepdims=True), (1, stat_width - columns))
     stage_second(0)
     for p in range(2):
@@ -353,7 +374,8 @@
 
     with scope("final"):
         cuts = [(0, 6), (6, 7), (7, 8)]
-        sums = [None] * len(cuts)
+        squares = [None] * len(cuts)
+        row_sums = []
         for i in range(tiles):
             r = pl.ds(i * TILE, TILE)
             row_sum = 0.0
@@ -363,25 +385,46 @@
                 if e <= parts[0 if i < cut_row else 1][3]:
                     terms += [rz[1, r, l], rz[5, r, l]]
                 value = add(*terms)
-                summed[r, l] = value
+                sums[r, l] = value.astype(bf16)
                 value = value * value
                 row_sum = row_sum + jnp.sum(value, axis=1, keepdims=True)
-                sums[k] = value if sums[k] is None else sums[k] + value
-            own[r, :] = row_sum
-        for (d, e), value in zip(cuts, sums):
+                squares[k] = value if squares[k] is None else squares[k] + value
+            scale[0, r, :] = row_sum
+        for (d, e), value in zip(cuts, squares):
             st[:, pl.ds(d * lane, (e - d) * lane)] = jnp.sum(value, axis=0, keepdims=True)
 
     me = gx * 2 + y
     for peer in plane:
         rdma(st, st1.at[me], s1s, s1r, peer).start()
     st1[me] = st[...]
+    diagonal = lax.broadcasted_iota(jnp.int32, (rows, rows), 0) == lax.broadcasted_iota(jnp.int32, (rows, rows), 1)
+
+    def turned(vector, axis):
+        return jnp.sum(jnp.where(diagonal, jnp.broadcast_to(vector, (rows, rows)), 0.0), axis=axis, keepdims=True)
+
+    info[0, 1:2, :] = turned(scale[0], 0)
+
+    def send_info(slot, peer):
+        rdma(info.at[0], info.at[slot], ins, inr.at[slot], peer).start()
+
+    send_info(X, x_peer)
+    send_info(Y, y_peer)
+    send_info(NEAR, near)
+    on_inner(lambda: send_info(MIDDLE, middle))
+    send_plane(sums, sums_of, False)
+    send_plane(params, params_of, True)
+    send_plane(sums, sums_of, True)
+
+    def send_sums(p):
+        send_near(sums, sums_of, NEAR, near, parts[p:p + 1])
+        on_inner(lambda: send_near(sums, sums_of, MIDDLE, middle, parts[p:p + 1]))
+
+    send_sums(0)
     take_send(cr, cs)
     take_send(some(3 * area(halves)), fs.at[0])
     take_send(some(9 * area(parts)), fs.at[1])
     take_send(some(3 * area(parts)), zs)
     take_send(some(12 * area(strips)), ks)
-    diagonal = lax.broadcasted_iota(jnp.int32, (rows, rows), 0) == lax.broadcasted_iota(jnp.int32, (rows, rows), 1)
-    state_down = jnp.sum(jnp.where(diagonal, jnp.broadcast_to(row_state[...], (rows, rows)), 0.0), axis=1, keepdims=True)
     with scope("stat1"):
         take_recv(st1.at[0:nx * 2 - 1], s1r)
     total = st1[0]
@@ -390,6 +433,7 @@
     tot[...] = total
     for t in range(1, nz):
         rdma(tot, st2.at[z], s2s, s2r, (gx, zof(t), y)).start()
+    send_sums(1)
     st2[z] = total
     with scope("stat2"):
         take_recv(st2.at[0:nz - 1], s2r)
@@ -404,15 +448,26 @@
     square_factor = factor * factor
     column_next = beta_two * col_state[...] + (1.0 - beta_two) * (square_factor * column_sum / full_width)
     row_average = (beta_two * state_sum + (1.0 - beta_two) * (square_factor * norm_square / columns)) / full_width
-    row_next = beta_two * state_down + (1.0 - beta_two) * (square_factor * own[...] / columns)
-    own[...] = (step_size * factor) / jnp.sqrt(row_next / row_average)
     col_scale = 1.0 / jnp.sqrt(column_next)
 
-    def update(r, l, _):
-        new = params[r, l].astype(f32) - (summed[r, l] * own[r, :]) * col_scale
-        full[x, c, z, y, r, l] = new.astype(bf16)
-    with scope("update"):
-        over(whole, update)
+    def next_of(slot):
+        return beta_two * info[slot, 0:1, :] + (1.0 - beta_two) * (square_factor * info[slot, 1:2, :] / columns)
+
+    def rate(slot):
+        if slot:
+            with scope(f"info{slot}"):
+                take_recv(info.at[slot], inr.at[slot])
+        scale[slot] = turned((step_size * factor) / jnp.sqrt(next_of(slot) / row_average), 1)
+
+    def update(slot, bx, u, by, regions):
+        def step(r, l, _):
+            new = params_of[slot, r, l].astype(f32) - (sums_of[slot, r, l].astype(f32) * scale[slot, r, :]) * col_scale_of(l)
+            full[bx, c, u, by, r, l] = new.astype(bf16)
+        for region in regions:
+            over(region, step)
+
+    def col_scale_of(l):
+        return col_scale[:, l.start:l.start + l.size]
 
     def same(view, ssem, rsem, peer):
         rdma(view, view, ssem, rsem, peer).start()
@@ -482,24 +537,42 @@
             take_recv(some(4 * area(strips)), gkr.at[t])
         each_strip(t, gcs, gcr, core_peer)
 
-    pass_far(0, 1, near)
-    send_q1(0)
-    on_inner(lambda: pass_far(0, 2, middle))
-    send_q2(0)
+    low, high = halves
+    rate(X)
+    rate(Y)
+    with scope("plane1"):
+        take_recv(some(4 * area(halves[:1])), nr.at[0])
+    update(Y, x, z, 1 - y, [low])
+    update(X, 1 - x, z, y, [high])
+    same(piece(x, z, 1 - y, low), moves(0), q3r.at[0], x_peer)
+    same(piece(1 - x, z, y, high), moves(0), q3r.at[0], y_peer)
+    rate(NEAR)
+    with scope("near"):
+        take_recv(some(2 * area(parts)), nzr.at[0])
+    update(NEAR, x, origin[1], y, parts)
+    on_inner(lambda: pass_far(1, 3, middle))
+    send_own(1)
+
+    @on_inner
+    def _():
+        rate(MIDDLE)
+        with scope("middle"):
+            take_recv(some(2 * area(parts)), nzr.at[1])
+        update(MIDDLE, x, origin[2], y, parts)
+        pass_far(2, 2, near)
+
+    rate(0)
+    update(0, x, z, y, [whole])
+    pass_core(0, x, y)
     new_ref[...] = full[x, c, z, y]
     col_ref[...] = column_next
-    row_ref[...] = jnp.sum(jnp.where(diagonal, jnp.broadcast_to(row_next, (rows, rows)), 0.0), axis=0, keepdims=True)
-    gather_cross(0)
-    take_z(1)
-    on_inner(lambda: pass_far(1, 3, middle))
-    send_own(1)
-
-    @on_inner
-    def _():
-        take_z(2)
-        pass_far(2, 2, near)
-
-    gather_side(0)
+    row_ref[...] = next_of(0)
+    with scope("plane2"):
+        take_recv(some(4 * area(halves[:1])), nr.at[1])
+    update(X, 1 - x, z, y, [low])
+    update(Y, x, z, 1 - y, [high])
+    pass_core(0, 1 - x, y)
+    pass_core(0, x, 1 - y)
     gather_far(0)
     pass_strip(0, 1, near)
     on_inner(lambda: pass_strip(0, 2, middle))
@@ -533,26 +606,30 @@
         take_strip(3)
         pass_strip(3, 3, near)
 
-    on_end(lambda: take_strip(2))
     gather_cross(3)
     gather_side(3)
+    on_end(lambda: take_strip(2))
     gather_far(3)
     on_end(lambda: take_strip(3))
 
     with scope("finish"):
         take_send(st1.at[0:nx * 2 - 1], s1s)
         take_send(st2.at[0:nz - 1], s2s)
-        take_send(some(3 * area(halves)), qs.at[0])
+        take_send(some(area(halves)), qs.at[0])
         take_send(some(9 * area(parts)), qs.at[1])
+        take_send(some(4 * area(halves)), ns)
 
         @on_end
         def _():
-            take_send(some(area(parts)), gzs)
+            take_send(some(2 * area(parts)), nzs)
+            take_send(info.at[0:3], ins)
             take_send(some(4 * area(strips)), gks)
 
         @on_inner
         def _():
-            take_send(some(5 * area(parts)), gzs)
+            take_send(some(4 * area(parts)), nzs)
+            take_send(info.at[0:4], ins)
+            take_send(some(3 * area(parts)), gzs)
             take_send(some(20 * area(strips)), gks)
 
         take_send(full.at[:, c], gcs)
@@ -595,18 +672,20 @@
             pltpu.VMEM((6, rows, columns), bf16),
             pltpu.VMEM((6, 2, 2, rows, 2 * lane), bf16),
             pltpu.VMEM((9 * 8 * (rows // TILE), TILE, lane), bf16),
-            pltpu.VMEM((rows, columns), f32),
-            pltpu.VMEM((rows, 1), f32),
+            pltpu.VMEM((5, rows, columns), bf16),
+            pltpu.VMEM((5, rows, columns), bf16),
+            pltpu.VMEM((5, 2, rows), f32),
+            pltpu.VMEM((5, rows, 1), f32),
             pltpu.VMEM((1, stat), f32),
             pltpu.VMEM((nx * 2, 1, stat), f32),
             pltpu.VMEM((1, stat), f32),
             pltpu.VMEM((nz, 1, stat), f32),
-            pltpu.VMEM((rows, columns), bf16),
             pltpu.VMEM((1, rows), f32),
             pltpu.VMEM((1, columns), f32),
             dma((nz,)), dma((3,)), one, dma((4,)), dma((nz,)), dma((2,)), dma((nz,)), dma((nz,)),
             one, dma((6, 2)), one, dma((6, 2)), one, one, one, one,
             one, dma((nz,)), dma((2,)), dma((nz,)), dma((nz,)), dma((nz,)), one, dma((nz,)), one, one,
+            one, dma((2,)), one, dma((2,)), one, dma((5,)),
         ],
         compiler_params=pltpu.CompilerParams(
             collective_id=0, has_side_effects=True, vmem_limit_bytes=VMEM_BYTES - held),

time: 74.6 us -> 72.4 us (0.971)
  Pallas kernels: 73.8 us -> 71.6 us
    pallas_call x1, Pallas kernels: 70.7 us -> 68.5 us  [fused(): pl.pallas_call(functools.partial(kernel, nx, nz), out_shape=tuple((pltpu....]
where the time goes in v5:
time: 72.4 us; the launch traced here: 72.2 us
  Pallas kernels  71.6 us (99%)
    pallas_call x1, Pallas kernels, fused(): pl.pallas_call(functools.partial(kernel, nx, nz), out_shape=tuple((pltpu....  68.5 us
    pallas_call x1, Pallas kernels, fused(): pl.pallas_call(functools.partial(write_out, nz), out_shape=tuple((jax.Sha...  3.06 us

profile of v5, /device:TPU:0, one launch (start us, length us, event | category | flops | bytes accessed | tf_op | source)
XLA Modules:
  0.0 72.2 jit_solution(18252769054316550571)
XLA Ops:
  0.6 68.5 %shard_map.75 = (bf16[112,1024]{1,0:T(8,128)(2,1)S(1)}, f32[1,112]{1,0:T(1,128)S(1)}, f32[1,1024]{1,0:T(1,128)S(1)}, bf16[2,2,4,2,112,1024]{5,4,3,2,1,0:T(8,128)(2,1)S(1)}) custom-call(bf16[2,2,4,2,112,1024]{5,4,3,2,1,0:T(8,128)(2,1)} %bitcast.4, bf16[112,1024]{1,0:T(8,128)(2,1)} %bitcast.5, f32[1,112]{1,0:T(1,128)} %row_in.1, f32[1,1024]{1,0:T(1,128)} %col_in.1), custom_call_target="tpu_custom_call" | custom-call | tf_op jit(solution)/shard_map/pallas_call | solution.py:663
  69.1 3.1 %shard_map.76 = (bf16[112,1024]{1,0:T(8,128)(2,1)}, f32[1,112]{1,0:T(1,128)}, f32[1,1024]{1,0:T(1,128)}, bf16[2,2,4,2,112,1024]{5,4,3,2,1,0:T(8,128)(2,1)}) custom-call(bf16[112,1024]{1,0:T(8,128)(2,1)S(1)} %get-tuple-element.12.new, f32[1,112]{1,0:T(1,128)S(1)} %get-tuple-element.13.row, f32[1,1024]{1,0:T(1,128)S(1)} %get-tuple-element.14.col, ...), custom_call_target="tpu_custom_call" | custom-call | tf_op jit(solution)/shard_map/pallas_call | solution.py:693

commit v6 on v5

--- a/solution.py
+++ b/solution.py
@@ -45,9 +45,9 @@
 
 
 def kernel(nx, nz, grad, params_in, row_in, col_in, new_ref, row_ref, col_ref, full,
-           lg, cr, rx, rz, rc, unit, sums_of, params_of, info, scale, st, st1, tot, st2, row_state, col_state,
+           lg, cr, rx, rz, rc, unit, sums_of, params_of, info, scale, state_down, sum_down, st, st1, tot, st2, row_state, col_state,
            lsem, isem, cs, cfr, cvr, fs, fr, hr, zs, zr, ks, kr, s1s, s1r, s2s, s2r,
-           gzs, gzr, qs, q1r, q2r, q3r, gks, gkr, gcs, gcr, ns, nr, nzs, nzr, ins, inr):
+           ns, nr, nzs, nzr, ins, inr):
     gx, z, y = lax.axis_index("gx"), lax.axis_index("gy"), lax.axis_index("gz")
     x, c = gx // 2, gx % 2
     rows, columns = new_ref.shape
@@ -63,10 +63,14 @@
     scope = jax.named_scope
     blocks = [(1 - x, 1 - y), (1 - x, y), (x, 1 - y), (x, y)]
 
+    def regions(cut, middle_lane):
+        return ([(0, cut, 0, 6), (cut, tiles, 0, 7)], [(0, cut, 6, 8), (cut, tiles, 7, 8)],
+                [(0, tiles, 0, middle_lane), (0, tiles, middle_lane, 8)])
+
+    out_row = (tiles * 4 + 3) // 7
     cut_row = (tiles * 4 + 3) // 7
-    parts = [(0, cut_row, 0, 6), (cut_row, tiles, 0, 7)]
-    strips = [(0, cut_row, 6, 8), (cut_row, tiles, 7, 8)]
-    halves = [(0, tiles, 0, 4), (0, tiles, 4, 8)]
+    parts, strips, halves = regions(cut_row, 4)
+    out_parts, out_strips, out_halves = regions(out_row, 4)
 
     def area(regions):
         return sum((b - a) * (e - d) for a, b, d, e in regions)
@@ -129,9 +133,9 @@
 
     X, Y, NEAR, MIDDLE = 1, 2, 3, 4
 
-    def send_plane(src, dst, swap):
-        for region, (slot, peer) in zip(halves, [(X, x_peer), (Y, y_peer)] if swap else [(Y, y_peer), (X, x_peer)]):
-            r, l = at(region)
+    def send_plane(src, dst, swap, a=0, b=tiles):
+        for region, (slot, peer) in zip(out_halves, [(X, x_peer), (Y, y_peer)] if swap else [(Y, y_peer), (X, x_peer)]):
+            r, l = at((a, b) + region[2:])
             rdma(src.at[r, l], dst.at[slot, r, l], ns, nr.at[1 if swap else 0], peer).start()
 
     def send_near(src, dst, slot, peer, regions):
@@ -139,10 +143,16 @@
             r, l = at(region)
             rdma(src.at[r, l], dst.at[slot, r, l], nzs, nzr.at[slot - NEAR], peer).start()
 
-    @on_inner
-    def _():
-        send_near(params_in, params_of, NEAR, near, parts)
-        send_near(params_in, params_of, MIDDLE, middle, parts)
+    early = out_row
+    if early:
+        send_plane(params_in, params_of, True, 0, early)
+
+    @on_inner
+    def _():
+        send_near(params_in, params_of, NEAR, near, out_parts)
+        send_near(params_in, params_of, MIDDLE, middle, out_parts)
+
+    on_end(lambda: send_near(params_in, params_of, NEAR, near, out_parts[1:]))
 
     def add(*terms):
         total = terms[0].astype(f32)
@@ -360,7 +370,7 @@
         pass_far_sum(1)
         pass_near_sum(1)
 
-    on_end(lambda: send_near(params, params_of, NEAR, near, parts))
+    on_end(lambda: send_near(params, params_of, NEAR, near, out_parts[:1]))
     info[0, 0:1, :] = row_state[...]
     st[:, columns:] = jnp.broadcast_to(jnp.sum(row_state[...], axis=1, keepdims=True), (1, stat_width - columns))
     stage_second(0)
@@ -389,7 +399,7 @@
                 value = value * value
                 row_sum = row_sum + jnp.sum(value, axis=1, keepdims=True)
                 squares[k] = value if squares[k] is None else squares[k] + value
-            scale[0, r, :] = row_sum
+            sum_down[0, r, :] = row_sum
         for (d, e), value in zip(cuts, squares):
             st[:, pl.ds(d * lane, (e - d) * lane)] = jnp.sum(value, axis=0, keepdims=True)
 
@@ -402,7 +412,7 @@
     def turned(vector, axis):
         return jnp.sum(jnp.where(diagonal, jnp.broadcast_to(vector, (rows, rows)), 0.0), axis=axis, keepdims=True)
 
-    info[0, 1:2, :] = turned(scale[0], 0)
+    info[0, 1:2, :] = turned(sum_down[0], 0)
 
     def send_info(slot, peer):
         rdma(info.at[0], info.at[slot], ins, inr.at[slot], peer).start()
@@ -412,14 +422,15 @@
     send_info(NEAR, near)
     on_inner(lambda: send_info(MIDDLE, middle))
     send_plane(sums, sums_of, False)
-    send_plane(params, params_of, True)
+    if early < tiles:
+        send_plane(params, params_of, True, early, tiles)
     send_plane(sums, sums_of, True)
 
-    def send_sums(p):
-        send_near(sums, sums_of, NEAR, near, parts[p:p + 1])
-        on_inner(lambda: send_near(sums, sums_of, MIDDLE, middle, parts[p:p + 1]))
-
-    send_sums(0)
+    def send_sums(pieces):
+        send_near(sums, sums_of, NEAR, near, pieces)
+        on_inner(lambda: send_near(sums, sums_of, MIDDLE, middle, pieces))
+
+    send_sums([out_parts[0]] + ([(out_row, tiles - 1, 0, 7)] if out_row < tiles - 1 else []))
     take_send(cr, cs)
     take_send(some(3 * area(halves)), fs.at[0])
     take_send(some(9 * area(parts)), fs.at[1])
@@ -433,8 +444,19 @@
     tot[...] = total
     for t in range(1, nz):
         rdma(tot, st2.at[z], s2s, s2r, (gx, zof(t), y)).start()
-    send_sums(1)
+    send_sums([(tiles - 1, tiles, 0, 7)])
     st2[z] = total
+    state_down[0] = turned(row_state[...], 1)
+
+    def turn_info(slot):
+        with scope(f"info{slot}"):
+            take_recv(info.at[slot], inr.at[slot])
+        state_down[slot] = turned(info[slot, 0:1, :], 1)
+        sum_down[slot] = turned(info[slot, 1:2, :], 1)
+
+    for slot in (X, Y, NEAR):
+        turn_info(slot)
+    on_inner(lambda: turn_info(MIDDLE))
     with scope("stat2"):
         take_recv(st2.at[0:nz - 1], s2r)
     total = st2[0]
@@ -450,14 +472,11 @@
     row_average = (beta_two * state_sum + (1.0 - beta_two) * (square_factor * norm_square / columns)) / full_width
     col_scale = 1.0 / jnp.sqrt(column_next)
 
-    def next_of(slot):
-        return beta_two * info[slot, 0:1, :] + (1.0 - beta_two) * (square_factor * info[slot, 1:2, :] / columns)
+    def next_of(state, total):
+        return beta_two * state + (1.0 - beta_two) * (square_factor * total / columns)
 
     def rate(slot):
-        if slot:
-            with scope(f"info{slot}"):
-                take_recv(info.at[slot], inr.at[slot])
-        scale[slot] = turned((step_size * factor) / jnp.sqrt(next_of(slot) / row_average), 1)
+        scale[slot] = (step_size * factor) / jnp.sqrt(next_of(state_down[slot], sum_down[slot]) / row_average)
 
     def update(slot, bx, u, by, regions):
         def step(r, l, _):
@@ -469,6 +488,10 @@
     def col_scale_of(l):
         return col_scale[:, l.start:l.start + l.size]
 
+    gzs, gzr, qs, q1r, q2r, q3r, gks, gcs = zs, cfr, fs, fr, hr, cvr, ks, cs
+    gcr = zr.at[0, 0]
+    parts, strips, halves = out_parts, out_strips, out_halves
+
     def same(view, ssem, rsem, peer):
         rdma(view, view, ssem, rsem, peer).start()
 
@@ -530,11 +553,11 @@
             same(full.at[:, c, origin[t], :, r, l], ssem, rsem, peer)
 
     def pass_strip(t, slot, peer):
-        each_strip(t, gks, gkr.at[slot], peer)
+        each_strip(t, gks, kr.at[slot, 0], peer)
 
     def take_strip(t):
         with scope(f"strip{t}"):
-            take_recv(some(4 * area(strips)), gkr.at[t])
+            take_recv(some(4 * area(strips)), kr.at[t, 0])
         each_strip(t, gcs, gcr, core_peer)
 
     low, high = halves
@@ -566,7 +589,7 @@
     pass_core(0, x, y)
     new_ref[...] = full[x, c, z, y]
     col_ref[...] = column_next
-    row_ref[...] = next_of(0)
+    row_ref[...] = next_of(info[0, 0:1, :], info[0, 1:2, :])
     with scope("plane2"):
         take_recv(some(4 * area(halves[:1])), nr.at[1])
     update(X, 1 - x, z, y, [low])
@@ -574,21 +597,25 @@
     pass_core(0, 1 - x, y)
     pass_core(0, x, 1 - y)
     gather_far(0)
+
+    @on_inner
+    def _():
+        pass_strip(0, 2, middle)
+        take_z(3)
+        pass_far(3, 3, near)
+
     pass_strip(0, 1, near)
-    on_inner(lambda: pass_strip(0, 2, middle))
     gather_cross(1)
     on_end(lambda: take_z(2))
     send_own(2)
-
-    @on_inner
-    def _():
-        take_z(3)
-        pass_far(3, 3, near)
-
     gather_side(1)
     gather_far(1)
-    take_strip(1)
-    on_inner(lambda: pass_strip(1, 3, middle))
+
+    @on_inner
+    def _():
+        take_strip(1)
+        pass_strip(1, 3, middle)
+
     gather_cross(2)
     on_end(lambda: take_z(3))
     send_own(3)
@@ -606,11 +633,12 @@
         take_strip(3)
         pass_strip(3, 3, near)
 
+    on_end(lambda: take_strip(1))
     gather_cross(3)
+    on_end(lambda: take_strip(2))
     gather_side(3)
-    on_end(lambda: take_strip(2))
+    on_end(lambda: take_strip(3))
     gather_far(3)
-    on_end(lambda: take_strip(3))
 
     with scope("finish"):
         take_send(st1.at[0:nx * 2 - 1], s1s)
@@ -676,6 +704,8 @@
             pltpu.VMEM((5, rows, columns), bf16),
             pltpu.VMEM((5, 2, rows), f32),
             pltpu.VMEM((5, rows, 1), f32),
+            pltpu.VMEM((5, rows, 1), f32),
+            pltpu.VMEM((5, rows, 1), f32),
             pltpu.VMEM((1, stat), f32),
             pltpu.VMEM((nx * 2, 1, stat), f32),
             pltpu.VMEM((1, stat), f32),
@@ -684,7 +714,6 @@
             pltpu.VMEM((1, columns), f32),
             dma((nz,)), dma((3,)), one, dma((4,)), dma((nz,)), dma((2,)), dma((nz,)), dma((nz,)),
             one, dma((6, 2)), one, dma((6, 2)), one, one, one, one,
-            one, dma((nz,)), dma((2,)), dma((nz,)), dma((nz,)), dma((nz,)), one, dma((nz,)), one, one,
             one, dma((2,)), one, dma((2,)), one, dma((5,)),
         ],
         compiler_params=pltpu.CompilerParams(

time: 72.4 us -> 71 us (0.981)
  Pallas kernels: 71.6 us -> 70.2 us
    pallas_call x1, Pallas kernels: 68.5 us -> 67.2 us  [fused(): pl.pallas_call(functools.partial(kernel, nx, nz), out_shape=tuple((pltpu....]
where the time goes in v6:
time: 71 us; the launch traced here: 70.9 us
  Pallas kernels  70.2 us (99%)
    pallas_call x1, Pallas kernels, fused(): pl.pallas_call(functools.partial(kernel, nx, nz), out_shape=tuple((pltpu....  67.2 us
    pallas_call x1, Pallas kernels, fused(): pl.pallas_call(functools.partial(write_out, nz), out_shape=tuple((jax.Sha...  3.06 us

profile of v6, /device:TPU:0, one launch (start us, length us, event | category | flops | bytes accessed | tf_op | source)
XLA Modules:
  0.0 70.9 jit_solution(10798188652774421587)
XLA Ops:
  0.6 67.2 %shard_map.75 = (bf16[112,1024]{1,0:T(8,128)(2,1)S(1)}, f32[1,112]{1,0:T(1,128)S(1)}, f32[1,1024]{1,0:T(1,128)S(1)}, bf16[2,2,4,2,112,1024]{5,4,3,2,1,0:T(8,128)(2,1)S(1)}) custom-call(bf16[2,2,4,2,112,1024]{5,4,3,2,1,0:T(8,128)(2,1)} %bitcast.4, bf16[112,1024]{1,0:T(8,128)(2,1)} %bitcast.5, f32[1,112]{1,0:T(1,128)} %row_in.1, f32[1,1024]{1,0:T(1,128)} %col_in.1), custom_call_target="tpu_custom_call" | custom-call | tf_op jit(solution)/shard_map/pallas_call | solution.py:691
  67.8 3.1 %shard_map.76 = (bf16[112,1024]{1,0:T(8,128)(2,1)}, f32[1,112]{1,0:T(1,128)}, f32[1,1024]{1,0:T(1,128)}, bf16[2,2,4,2,112,1024]{5,4,3,2,1,0:T(8,128)(2,1)}) custom-call(bf16[112,1024]{1,0:T(8,128)(2,1)S(1)} %get-tuple-element.12.new, f32[1,112]{1,0:T(1,128)S(1)} %get-tuple-element.13.row, f32[1,1024]{1,0:T(1,128)S(1)} %get-tuple-element.14.col, ...), custom_call_target="tpu_custom_call" | custom-call | tf_op jit(solution)/shard_map/pallas_call | solution.py:722

commit v7 on v6

--- a/solution.py
+++ b/solution.py
@@ -67,10 +67,10 @@
         return ([(0, cut, 0, 6), (cut, tiles, 0, 7)], [(0, cut, 6, 8), (cut, tiles, 7, 8)],
                 [(0, tiles, 0, middle_lane), (0, tiles, middle_lane, 8)])
 
-    out_row = (tiles * 4 + 3) // 7
     cut_row = (tiles * 4 + 3) // 7
     parts, strips, halves = regions(cut_row, 4)
-    out_parts, out_strips, out_halves = regions(out_row, 4)
+    out_parts, out_strips, out_halves = [(0, tiles, 0, 3), (0, tiles, 3, 6)], [(0, tiles, 6, 8)], halves
+    out_flat = [(0, tiles, 0, 6)]
 
     def area(regions):
         return sum((b - a) * (e - d) for a, b, d, e in regions)
@@ -86,7 +86,7 @@
         return flip(z, t, nz)
 
     inside = (z + z // 2) % 2
-    near, middle = (gx, zof(1), y), (gx, zof(3), y)
+    near, middle, far = (gx, zof(1), y), (gx, zof(3), y), (gx, zof(2), y)
     origin = [z, zof(1), flip(z, 2 + inside, nz), flip(z, 3 - inside, nz)]
 
     def on_end(step):
@@ -143,14 +143,14 @@
             r, l = at(region)
             rdma(src.at[r, l], dst.at[slot, r, l], nzs, nzr.at[slot - NEAR], peer).start()
 
-    early = out_row
+    early = (tiles * 4 + 3) // 7
     if early:
         send_plane(params_in, params_of, True, 0, early)
 
     @on_inner
     def _():
-        send_near(params_in, params_of, NEAR, near, out_parts)
-        send_near(params_in, params_of, MIDDLE, middle, out_parts)
+        send_near(params_in, params_of, NEAR, near, out_flat)
+        send_near(params_in, params_of, MIDDLE, middle, out_flat)
 
     on_end(lambda: send_near(params_in, params_of, NEAR, near, out_parts[1:]))
 
@@ -369,6 +369,7 @@
     def _():
         pass_far_sum(1)
         pass_near_sum(1)
+        send_near(params, params_of, MIDDLE, far, out_flat)
 
     on_end(lambda: send_near(params, params_of, NEAR, near, out_parts[:1]))
     info[0, 0:1, :] = row_state[...]
@@ -420,7 +421,12 @@
     send_info(X, x_peer)
     send_info(Y, y_peer)
     send_info(NEAR, near)
-    on_inner(lambda: send_info(MIDDLE, middle))
+
+    @on_inner
+    def _():
+        send_info(MIDDLE, middle)
+        send_info(MIDDLE, far)
+
     send_plane(sums, sums_of, False)
     if early < tiles:
         send_plane(params, params_of, True, early, tiles)
@@ -430,7 +436,8 @@
         send_near(sums, sums_of, NEAR, near, pieces)
         on_inner(lambda: send_near(sums, sums_of, MIDDLE, middle, pieces))
 
-    send_sums([out_parts[0]] + ([(out_row, tiles - 1, 0, 7)] if out_row < tiles - 1 else []))
+    late = (tiles * 3) // 7
+    send_sums([out_parts[0], (0, tiles - late, 3, 6)])
     take_send(cr, cs)
     take_send(some(3 * area(halves)), fs.at[0])
     take_send(some(9 * area(parts)), fs.at[1])
@@ -444,7 +451,9 @@
     tot[...] = total
     for t in range(1, nz):
         rdma(tot, st2.at[z], s2s, s2r, (gx, zof(t), y)).start()
-    send_sums([(tiles - 1, tiles, 0, 7)])
+    if late:
+        send_sums([(tiles - late, tiles, 3, 6)])
+    on_inner(lambda: send_near(sums, sums_of, MIDDLE, far, out_flat))
     st2[z] = total
     state_down[0] = turned(row_state[...], 1)
 
@@ -454,9 +463,8 @@
         state_down[slot] = turned(info[slot, 0:1, :], 1)
         sum_down[slot] = turned(info[slot, 1:2, :], 1)
 
-    for slot in (X, Y, NEAR):
+    for slot in (X, Y, NEAR, MIDDLE):
         turn_info(slot)
-    on_inner(lambda: turn_info(MIDDLE))
     with scope("stat2"):
         take_recv(st2.at[0:nz - 1], s2r)
     total = st2[0]
@@ -503,7 +511,7 @@
         return full.at[bx, c, u, by, r, l]
 
     def pass_core(t, bx, by):
-        for region in parts if t else [whole]:
+        for region in out_flat if t else [whole]:
             same(piece(bx, origin[t], by, region), gcs, gcr, core_peer)
 
     def send_q1(t):
@@ -522,7 +530,7 @@
         send_q2(t)
 
     def pass_far(t, slot, peer):
-        for region in parts:
+        for region in out_flat:
             same(piece(x, origin[t], y, region), gzs, gzr.at[slot], peer)
 
     def take_z(t):
@@ -547,18 +555,22 @@
             take_recv(some(area(spans(t))), q3r.at[t])
         pass_core(t, 1 - x, 1 - y)
 
-    def each_strip(t, ssem, rsem, peer):
-        for region in strips:
-            r, l = at(region)
-            same(full.at[:, c, origin[t], :, r, l], ssem, rsem, peer)
-
-    def pass_strip(t, slot, peer):
-        each_strip(t, gks, kr.at[slot, 0], peer)
-
-    def take_strip(t):
-        with scope(f"strip{t}"):
-            take_recv(some(4 * area(strips)), kr.at[t, 0])
-        each_strip(t, gcs, gcr, core_peer)
+    def each_strip(t, p, ssem, rsem, peer):
+        r, l = at(strips[0])
+        for bx, by in [(1 - x, 1 - y)] if p else [(x, y), (1 - x, y), (x, 1 - y)]:
+            same(full.at[bx, c, origin[t], by, r, l], ssem, rsem, peer)
+
+    def pass_strip(t, p, slot, peer):
+        each_strip(t, p, gks, kr.at[slot, p], peer)
+
+    def take_strip(t, p):
+        with scope(f"strip{t}_{p}"):
+            take_recv(some((1 if p else 3) * area(strips)), kr.at[t, p])
+        each_strip(t, p, gcs, gcr, core_peer)
+
+    def own_strip(p):
+        pass_strip(0, p, 1, near)
+        on_inner(lambda: pass_strip(0, p, 2, middle))
 
     low, high = halves
     rate(X)
@@ -576,14 +588,6 @@
     on_inner(lambda: pass_far(1, 3, middle))
     send_own(1)
 
-    @on_inner
-    def _():
-        rate(MIDDLE)
-        with scope("middle"):
-            take_recv(some(2 * area(parts)), nzr.at[1])
-        update(MIDDLE, x, origin[2], y, parts)
-        pass_far(2, 2, near)
-
     rate(0)
     update(0, x, z, y, [whole])
     pass_core(0, x, y)
@@ -594,50 +598,59 @@
         take_recv(some(4 * area(halves[:1])), nr.at[1])
     update(X, 1 - x, z, y, [low])
     update(Y, x, z, 1 - y, [high])
+    own_strip(0)
     pass_core(0, 1 - x, y)
     pass_core(0, x, 1 - y)
+    rate(MIDDLE)
+    with scope("middle"):
+        take_recv(some(2 * area(parts)), nzr.at[1])
+    update(MIDDLE, x, origin[2], y, parts)
     gather_far(0)
-
-    @on_inner
-    def _():
-        pass_strip(0, 2, middle)
+    own_strip(1)
+    gather_cross(1)
+    send_own(2)
+
+    @on_inner
+    def _():
         take_z(3)
         pass_far(3, 3, near)
 
-    pass_strip(0, 1, near)
-    gather_cross(1)
-    on_end(lambda: take_z(2))
-    send_own(2)
+    def relay_strip(t, p, slot, peer):
+        take_strip(t, p)
+        pass_strip(t, p, slot, peer)
+
+    on_inner(lambda: relay_strip(1, 0, 3, middle))
     gather_side(1)
     gather_far(1)
-
-    @on_inner
-    def _():
-        take_strip(1)
-        pass_strip(1, 3, middle)
-
+    on_inner(lambda: relay_strip(1, 1, 3, middle))
+
+    def pass_second():
+        relay_strip(2, 0, 2, near)
+        relay_strip(2, 1, 2, near)
+
+    pl.when((inside == 1) & (c == 0))(pass_second)
     gather_cross(2)
     on_end(lambda: take_z(3))
     send_own(3)
-
-    @on_inner
-    def _():
-        take_strip(2)
-        pass_strip(2, 2, near)
+    pl.when((inside == 1) & (c == 1))(pass_second)
+
+    @on_inner
+    def _():
+        relay_strip(3, 0, 3, near)
+        relay_strip(3, 1, 3, near)
 
     gather_side(2)
     gather_far(2)
 
-    @on_inner
-    def _():
-        take_strip(3)
-        pass_strip(3, 3, near)
-
-    on_end(lambda: take_strip(1))
+    def end_strip(t):
+        take_strip(t, 0)
+        take_strip(t, 1)
+
+    on_end(lambda: end_strip(1))
     gather_cross(3)
-    on_end(lambda: take_strip(2))
+    on_end(lambda: end_strip(2))
     gather_side(3)
-    on_end(lambda: take_strip(3))
+    on_end(lambda: end_strip(3))
     gather_far(3)
 
     with scope("finish"):
@@ -655,9 +668,9 @@
 
         @on_inner
         def _():
-            take_send(some(4 * area(parts)), nzs)
-            take_send(info.at[0:4], ins)
-            take_send(some(3 * area(parts)), gzs)
+            take_send(some(6 * area(parts)), nzs)
+            take_send(info, ins)
+            take_send(some(2 * area(parts)), gzs)
             take_send(some(20 * area(strips)), gks)
 
         take_send(full.at[:, c], gcs)

time: 71 us -> 69.9 us (0.985)
  Pallas kernels: 70.2 us -> 69.1 us
    pallas_call x1, Pallas kernels: 67.2 us -> 66.1 us  [fused(): pl.pallas_call(functools.partial(kernel, nx, nz), out_shape=tuple((pltpu....]
where the time goes in v7:
time: 69.9 us; the launch traced here: 69.8 us
  Pallas kernels  69.1 us (99%)
    pallas_call x1, Pallas kernels, fused(): pl.pallas_call(functools.partial(kernel, nx, nz), out_shape=tuple((pltpu....  66.1 us
    pallas_call x1, Pallas kernels, fused(): pl.pallas_call(functools.partial(write_out, nz), out_shape=tuple((jax.Sha...  3.06 us

profile of v7, /device:TPU:0, one launch (start us, length us, event | category | flops | bytes accessed | tf_op | source)
XLA Modules:
  0.0 69.8 jit_solution(4445297416980992789)
XLA Ops:
  0.6 66.1 %shard_map.75 = (bf16[112,1024]{1,0:T(8,128)(2,1)S(1)}, f32[1,112]{1,0:T(1,128)S(1)}, f32[1,1024]{1,0:T(1,128)S(1)}, bf16[2,2,4,2,112,1024]{5,4,3,2,1,0:T(8,128)(2,1)S(1)}) custom-call(bf16[2,2,4,2,112,1024]{5,4,3,2,1,0:T(8,128)(2,1)} %bitcast.4, bf16[112,1024]{1,0:T(8,128)(2,1)} %bitcast.5, f32[1,112]{1,0:T(1,128)} %row_in.1, f32[1,1024]{1,0:T(1,128)} %col_in.1), custom_call_target="tpu_custom_call" | custom-call | tf_op jit(solution)/shard_map/pallas_call | solution.py:704
  66.7 3.1 %shard_map.76 = (bf16[112,1024]{1,0:T(8,128)(2,1)}, f32[1,112]{1,0:T(1,128)}, f32[1,1024]{1,0:T(1,128)}, bf16[2,2,4,2,112,1024]{5,4,3,2,1,0:T(8,128)(2,1)}) custom-call(bf16[112,1024]{1,0:T(8,128)(2,1)S(1)} %get-tuple-element.12.new, f32[1,112]{1,0:T(1,128)S(1)} %get-tuple-element.13.row, f32[1,1024]{1,0:T(1,128)S(1)} %get-tuple-element.14.col, ...), custom_call_target="tpu_custom_call" | custom-call | tf_op jit(solution)/shard_map/pallas_call | solution.py:735

commit v8 on v7

--- a/solution.py
+++ b/solution.py
@@ -436,8 +436,7 @@
         send_near(sums, sums_of, NEAR, near, pieces)
         on_inner(lambda: send_near(sums, sums_of, MIDDLE, middle, pieces))
 
-    late = (tiles * 3) // 7
-    send_sums([out_parts[0], (0, tiles - late, 3, 6)])
+    send_sums(out_parts)
     take_send(cr, cs)
     take_send(some(3 * area(halves)), fs.at[0])
     take_send(some(9 * area(parts)), fs.at[1])
@@ -451,8 +450,6 @@
     tot[...] = total
     for t in range(1, nz):
         rdma(tot, st2.at[z], s2s, s2r, (gx, zof(t), y)).start()
-    if late:
-        send_sums([(tiles - late, tiles, 3, 6)])
     on_inner(lambda: send_near(sums, sums_of, MIDDLE, far, out_flat))
     st2[z] = total
     state_down[0] = turned(row_state[...], 1)
@@ -542,7 +539,7 @@
         with scope(f"q1_{t}"):
             take_recv(some(area(spans(t))), q1r.at[t])
         same(piece(x, u, 1 - y, a), moves(t), q3r.at[t], x_peer)
-        same(piece(1 - x, u, y, b), moves(t), q3r.at[t], y_peer)
+        same(piece(1 - x, u, y, b), moves(t), zr.at[0, 1] if t == 3 else q3r.at[t], y_peer)
 
     def gather_side(t):
         with scope(f"q2_{t}"):
@@ -601,13 +598,18 @@
     own_strip(0)
     pass_core(0, 1 - x, y)
     pass_core(0, x, 1 - y)
-    rate(MIDDLE)
-    with scope("middle"):
-        take_recv(some(2 * area(parts)), nzr.at[1])
-    update(MIDDLE, x, origin[2], y, parts)
+
+    def update_middle():
+        rate(MIDDLE)
+        with scope("middle"):
+            take_recv(some(2 * area(parts)), nzr.at[1])
+        update(MIDDLE, x, origin[2], y, parts)
+
+    on_inner(update_middle)
     gather_far(0)
     own_strip(1)
     gather_cross(1)
+    on_end(update_middle)
     send_own(2)
 
     @on_inner
@@ -651,7 +653,10 @@
     on_end(lambda: end_strip(2))
     gather_side(3)
     on_end(lambda: end_strip(3))
-    gather_far(3)
+    for span, sem in zip(spans(3), (q3r.at[3], zr.at[0, 1])):
+        with scope(f"q3_3_{span[2]}"):
+            take_recv(some(area([span])), sem)
+        same(piece(1 - x, origin[3], 1 - y, span), gcs, gcr, core_peer)
 
     with scope("finish"):
         take_send(st1.at[0:nx * 2 - 1], s1s)

time: 69.9 us -> 69.6 us (level)
  no operation moved by 1% of the time
where the time goes in v8:
time: 69.6 us; the launch traced here: 69.5 us
  Pallas kernels  68.8 us (99%)
    pallas_call x1, Pallas kernels, fused(): pl.pallas_call(functools.partial(kernel, nx, nz), out_shape=tuple((pltpu....  65.8 us
    pallas_call x1, Pallas kernels, fused(): pl.pallas_call(functools.partial(write_out, nz), out_shape=tuple((jax.Sha...  3.06 us

profile of v8, /device:TPU:0, one launch (start us, length us, event | category | flops | bytes accessed | tf_op | source)
XLA Modules:
  0.0 69.5 jit_solution(5100429212069371236)
XLA Ops:
  0.6 65.8 %shard_map.75 = (bf16[112,1024]{1,0:T(8,128)(2,1)S(1)}, f32[1,112]{1,0:T(1,128)S(1)}, f32[1,1024]{1,0:T(1,128)S(1)}, bf16[2,2,4,2,112,1024]{5,4,3,2,1,0:T(8,128)(2,1)S(1)}) custom-call(bf16[2,2,4,2,112,1024]{5,4,3,2,1,0:T(8,128)(2,1)} %bitcast.4, bf16[112,1024]{1,0:T(8,128)(2,1)} %bitcast.5, f32[1,112]{1,0:T(1,128)} %row_in.1, f32[1,1024]{1,0:T(1,128)} %col_in.1), custom_call_target="tpu_custom_call" | custom-call | tf_op jit(solution)/shard_map/pallas_call | solution.py:709
  66.4 3.1 %shard_map.76 = (bf16[112,1024]{1,0:T(8,128)(2,1)}, f32[1,112]{1,0:T(1,128)}, f32[1,1024]{1,0:T(1,128)}, bf16[2,2,4,2,112,1024]{5,4,3,2,1,0:T(8,128)(2,1)}) custom-call(bf16[112,1024]{1,0:T(8,128)(2,1)S(1)} %get-tuple-element.12.new, f32[1,112]{1,0:T(1,128)S(1)} %get-tuple-element.13.row, f32[1,1024]{1,0:T(1,128)S(1)} %get-tuple-element.14.col, ...), custom_call_target="tpu_custom_call" | custom-call | tf_op jit(solution)/shard_map/pallas_call | solution.py:740

commit v9 on v8

--- a/solution.py
+++ b/solution.py
@@ -110,7 +110,7 @@
         return unit.at[pl.ds(0, count)]
 
     first = 3
-    loads = {t: pltpu.make_async_copy(grad.at[:, c, zof(t)], lg.at[t], lsem.at[t]) for t in (3, 2, 1, 0)}
+    loads = {t: pltpu.make_async_copy(grad.at[:, c, zof(t)], lg.at[t], lsem.at[0 if t == 3 else 1]) for t in (3, 2, 1, 0)}
     for t in loads:
         loads[t].start()
     small = [pltpu.make_async_copy(src, dst, isem.at[k]) for k, (src, dst) in enumerate(
@@ -203,7 +203,7 @@
         for region in strips:
             r, l = at(region)
             _, m = at(region, 6)
-            rdma(lg.at[t, side[h], :, r, l], rc.at[slot, h, :, r, m], ks, kr.at[slot, h], peer).start()
+            rdma(lg.at[t, side[h], :, r, l], rc.at[slot, h, :, r, m], ks, kr.at[max(slot, 1) - 1, h], peer).start()
 
     def send_strips(t, slot, peer):
         for h in range(2):
@@ -212,7 +212,7 @@
     def take_strips(h, *slots):
         for slot in slots:
             with scope(f"line{slot}_{h}"):
-                take_recv(some(2 * area(strips)), kr.at[slot, h])
+                take_recv(some(2 * area(strips)), kr.at[max(slot, 1) - 1, h])
 
     def strip_add(t, h, *slots):
         for by in range(2):
@@ -231,7 +231,8 @@
     def stage_pair(t):
         with scope(f"pair{t}"):
             take_recv(cr.at[t], cvr.at[t])
-            loads[t].wait()
+            if t == 2:
+                take_recv(lg.at[0:3], lsem.at[1])
             for bx, by in blocks:
                 pair_sum(t, bx, by)
 
@@ -416,7 +417,7 @@
     info[0, 1:2, :] = turned(sum_down[0], 0)
 
     def send_info(slot, peer):
-        rdma(info.at[0], info.at[slot], ins, inr.at[slot], peer).start()
+        rdma(info.at[0], info.at[slot], ins, inr.at[max(slot - Y, 0)], peer).start()
 
     send_info(X, x_peer)
     send_info(Y, y_peer)
@@ -456,7 +457,10 @@
 
     def turn_info(slot):
         with scope(f"info{slot}"):
-            take_recv(info.at[slot], inr.at[slot])
+            if slot == X:
+                take_recv(info.at[X:NEAR], inr.at[0])
+            elif slot > Y:
+                take_recv(info.at[slot], inr.at[slot - Y])
         state_down[slot] = turned(info[slot, 0:1, :], 1)
         sum_down[slot] = turned(info[slot, 1:2, :], 1)
 
@@ -558,11 +562,11 @@
             same(full.at[bx, c, origin[t], by, r, l], ssem, rsem, peer)
 
     def pass_strip(t, p, slot, peer):
-        each_strip(t, p, gks, kr.at[slot, p], peer)
+        each_strip(t, p, gks, kr.at[slot - 1, p], peer)
 
     def take_strip(t, p):
         with scope(f"strip{t}_{p}"):
-            take_recv(some((1 if p else 3) * area(strips)), kr.at[t, p])
+            take_recv(some((1 if p else 3) * area(strips)), kr.at[t - 1, p])
         each_strip(t, p, gcs, gcr, core_peer)
 
     def own_strip(p):
@@ -730,9 +734,9 @@
             pltpu.VMEM((nz, 1, stat), f32),
             pltpu.VMEM((1, rows), f32),
             pltpu.VMEM((1, columns), f32),
-            dma((nz,)), dma((3,)), one, dma((4,)), dma((nz,)), dma((2,)), dma((nz,)), dma((nz,)),
-            one, dma((6, 2)), one, dma((6, 2)), one, one, one, one,
-            one, dma((2,)), one, dma((2,)), one, dma((5,)),
+            dma((2,)), dma((3,)), one, dma((4,)), dma((nz,)), dma((2,)), dma((nz,)), dma((nz,)),
+            one, dma((6, 2)), one, dma((5, 2)), one, one, one, one,
+            one, dma((2,)), one, dma((2,)), one, dma((3,)),
         ],
         compiler_params=pltpu.CompilerParams(
             collective_id=0, has_side_effects=True, vmem_limit_bytes=VMEM_BYTES - held),

time: 69.6 us -> 69.6 us (level)
  no operation moved by 1% of the time
where the time goes in v9:
time: 69.6 us; the launch traced here: 69.4 us
  Pallas kernels  68.8 us (99%)
    pallas_call x1, Pallas kernels, fused(): pl.pallas_call(functools.partial(kernel, nx, nz), out_shape=tuple((pltpu....  65.7 us
    pallas_call x1, Pallas kernels, fused(): pl.pallas_call(functools.partial(write_out, nz), out_shape=tuple((jax.Sha...  3.06 us

profile of v9, /device:TPU:0, one launch (start us, length us, event | category | flops | bytes accessed | tf_op | source)
XLA Modules:
  0.0 69.4 jit_solution(8249290872664319173)
XLA Ops:
  0.6 65.7 %shard_map.75 = (bf16[112,1024]{1,0:T(8,128)(2,1)S(1)}, f32[1,112]{1,0:T(1,128)S(1)}, f32[1,1024]{1,0:T(1,128)S(1)}, bf16[2,2,4,2,112,1024]{5,4,3,2,1,0:T(8,128)(2,1)S(1)}) custom-call(bf16[2,2,4,2,112,1024]{5,4,3,2,1,0:T(8,128)(2,1)} %bitcast.4, bf16[112,1024]{1,0:T(8,128)(2,1)} %bitcast.5, f32[1,112]{1,0:T(1,128)} %row_in.1, f32[1,1024]{1,0:T(1,128)} %col_in.1), custom_call_target="tpu_custom_call" | custom-call | tf_op jit(solution)/shard_map/pallas_call | solution.py:713
  66.3 3.1 %shard_map.76 = (bf16[112,1024]{1,0:T(8,128)(2,1)}, f32[1,112]{1,0:T(1,128)}, f32[1,1024]{1,0:T(1,128)}, bf16[2,2,4,2,112,1024]{5,4,3,2,1,0:T(8,128)(2,1)}) custom-call(bf16[112,1024]{1,0:T(8,128)(2,1)S(1)} %get-tuple-element.12.new, f32[1,112]{1,0:T(1,128)S(1)} %get-tuple-element.13.row, f32[1,1024]{1,0:T(1,128)S(1)} %get-tuple-element.14.col, ...), custom_call_target="tpu_custom_call" | custom-call | tf_op jit(solution)/shard_map/pallas_call | solution.py:744
